TPU v7x, 512 devices: a whole 4x4x16 slice. The times are simulated.
512 devices in a mesh: row: 16 (over z), col: 32 (over y, x, core).
Axes of the slice: x: 4, y: 4, z: 16, core: 2. Of those that a mesh axis runs over, the one named last changes fastest.
Arguments:
- weight_basis: float32 [16384, 16384], P('row', 'col'), may hold values from -6 to 6
- panels: float32 [16384, 1024], P(('row', 'col')), may hold values from -1 to 1, as said below
- factors: float32 [256, 1024], P('col'), as said below
Outputs:
- rotated: float32 [16384, 16384], P('row', 'col')
Inputs may be any that keep to these rules, and one draw needn't show every extreme that they name: Column k of panels is zero above row k and one at row k. Columns b * 256 to (b + 1) * 256 - 1 of factors hold an upper triangular T_b for which I - V_b T_b transpose(V_b) is orthogonal.
All inputs are finite; a program needn't handle non-finite values.
Results may differ from a plain program's by a relative error of at most 0.00012.
Values sent between devices are 32-bit elements; how exact they have to be, the bound alone decides.
No kernel may reach another device: no remote copies, remote signals or barrier semaphores. Data moves between devices by JAX's collectives and lax.ppermute only.
A program may use at most 64 MiB of HBM per device.

v0:
```python
import jax
import jax.numpy as jnp
from jax import lax
from jax.sharding import PartitionSpec as P


def cut_along(array, dim, size):
    before, after = (array.shape[:dim], array.shape[dim + 1 :])
    return jnp.moveaxis(array.reshape(*before, size, -1, *after), dim, 0)


def summed_on_arrival(array, axis, dim):
    parts = cut_along(array, dim, lax.axis_size(axis))
    arrived = lax.all_to_all(parts, axis, split_axis=0, concat_axis=0, tiled=True)
    return arrived.sum(axis=0)


def joined_along(parts, dim):
    parts = jnp.moveaxis(parts, 0, dim)
    shape = parts.shape
    return parts.reshape(*shape[:dim], shape[dim] * shape[dim + 1], *shape[dim + 2 :])


def gather_together(arrays, axis, dims):
    line = jnp.concatenate([a.reshape(-1) for a in arrays])
    lines, at, gathered = (lax.all_gather(line, axis), 0, [])
    for a, dim in zip(arrays, dims):
        parts = lines[:, at : at + a.size].reshape(-1, *a.shape)
        gathered.append(joined_along(parts, dim))
        at += a.size
    return tuple(gathered)


def settle(partial_value, triangle):
    exact = lax.Precision.HIGHEST
    portion = summed_on_arrival(partial_value, "row", 1)
    local_applied = jnp.dot(triangle, portion, precision=exact)
    return lax.all_gather(local_applied, "row", axis=1, tiled=True)


def per_device(weight_basis, panels, factors):
    exact = lax.Precision.HIGHEST
    panel_rows, triangles = gather_together((panels, factors), "col", (0, 0))
    block_width = triangles.shape[0]
    blocks_in = triangles.shape[1] // block_width
    current = weight_basis
    for block in reversed(range(blocks_in)):
        lower = block * block_width
        vblock = panel_rows[:, lower : lower + block_width]
        partial_value = jnp.dot(vblock.T, current, precision=exact)
        applied = settle(partial_value, triangles[:, lower : lower + block_width])
        current = current - jnp.dot(vblock, applied, precision=exact)
    return current


def solution(mesh):
    placed = (P("row", "col"), P(("row", "col"), None), P("col", None))
    return jax.shard_map(
        per_device, mesh=mesh, in_specs=placed, out_specs=P("row", "col"), check_vma=False
    )
```

profile of v0, /device:TPU:6, one launch (start us, length us, event | category | flops | bytes accessed | tf_op | source)
XLA Modules:
  0.0 389.3 jit_solution(11837946859424070882)
XLA Ops:
  6.5 0.0 all-gather.3.cloned.1.call-start
  6.5 0.8 copy.19
  7.3 0.9 copy.16
  8.2 0.7 pad_maximum_fusion
  8.9 0.0 all-gather.3.cloned.1.call-update
  8.9 68.0 %all-gather.3.cloned.1.call-done = f32[1310720]{0:T(1024)} async-done(((f32[40960]{0:T(1024)}), f32[1310720]{0:T(1024)}) %all-gather.3.cloned.1.call-update) | async-done | bytes 5242896 | tf_op jit(solution)/shard_map/all_gather | solution.py:26
  76.9 5.6 %reshape.24 = f32[32,40960]{1,0:T(8,128)} reshape(f32[1310720]{0:T(1024)} %all-gather.3.cloned.1.call-done) | data formatting | bytes 10485760 | tf_op jit(solution)/shard_map/all_gather | solution.py:26
  82.5 4.5 %slice.40 = f32[32,32768]{1,0:T(8,128)} slice(f32[32,40960]{1,0:T(8,128)} %reshape.24), slice={[0:32], [0:32768]} | slice | bytes 8388608 | tf_op jit(solution)/shard_map/slice | solution.py:28
  87.1 0.0 copy-start.1
  87.1 5.2 %reshape_reshape.6 = f32[1024,1024]{1,0:T(8,128)} reshape(f32[32,32768]{1,0:T(8,128)} %slice.40) | data formatting | bytes 8388608 | tf_op jit(solution)/shard_map/reshape;reshape | solution.py:21
  92.2 0.0 copy-done.1
  92.2 5.5 %fusion.10 = f32[256,512]{0,1:T(8,128)} fusion(f32[1024,512]{1,0:T(8,128)S(1)} %copy-done.1, f32[1024,1024]{1,0:T(8,128)} %reshape_reshape.6), kind=kOutput, calls=%fused_computation.14 | convolution fusion | flops 1610612736 | bytes 3670016 | tf_op jit(solution)/shard_map/dot_general | solution.py:50
  97.7 0.0 slice-start
  97.7 12.4 %all-to-all-start = ((f32[16,256,32]{1,2,0:T(8,128)}), f32[16,256,32]{1,2,0:T(8,128)S(1)}, u32[]{:S(2)}, u32[]{:S(2)}) async-start(f32[16,256,32]{1,2,0:T(8,128)} %bitcast.1), calls=%async_computation | async-start | bytes 1048576 | tf_op jit(solution)/shard_map/all_to_all | solution.py:14
  110.1 0.0 slice-done
  110.1 0.2 reshape_reshape.7
  110.3 29.0 %all-to-all-done = f32[16,256,32]{1,2,0:T(8,128)S(1)} async-done(((f32[16,256,32]{1,2,0:T(8,128)}), f32[16,256,32]{1,2,0:T(8,128)S(1)}, u32[]{:S(2)}, u32[]{:S(2)}) %all-to-all-start) | async-done | bytes 524320 | tf_op jit(solution)/shard_map/all_to_all | solution.py:14
  139.4 0.3 fusion.18
  139.8 33.6 %all_gather.20 = f32[256,512]{0,1:T(8,128)S(1)} all-gather(f32[256,32]{0,1:T(8,128)S(1)} %fusion.18), channel_id=1, replica_groups=mesh['row'=16,'col'=32] {'row'}, dimensions={1}, use_global_device_ids=true | all-gather | bytes 557056 | tf_op jit(solution)/shard_map/all_gather | solution.py:38
  173.4 3.8 convolution_subtract_fusion.3
  177.2 4.7 %fusion.7 = f32[256,512]{0,1:T(8,128)S(1)} fusion(f32[1024,512]{1,0:T(8,128)S(1)} %convolution_subtract_fusion.3, f32[1024,1024]{1,0:T(8,128)} %reshape_reshape.6), kind=kOutput, calls=%fused_computation.11 | convolution fusion | flops 1610612736 | bytes 3670016 | tf_op jit(solution)/shard_map/dot_general | solution.py:50
  181.8 25.9 %all_to_all.20 = f32[16,256,32]{1,2,0:T(8,128)} all-to-all(f32[16,256,32]{1,2,0:T(8,128)S(1)} %bitcast.30), channel_id=1, replica_groups=mesh['row'=16,'col'=32] {'row'}, dimensions={0} | all-to-all | bytes 1048576 | tf_op jit(solution)/shard_map/all_to_all | solution.py:14
  207.8 1.1 reduce_sum.37
  208.8 0.3 fusion.16
  209.2 33.3 %all_gather.21 = f32[256,512]{0,1:T(8,128)S(1)} all-gather(f32[256,32]{0,1:T(8,128)S(1)} %fusion.16), channel_id=1, replica_groups=mesh['row'=16,'col'=32] {'row'}, dimensions={1}, use_global_device_ids=true | all-gather | bytes 557056 | tf_op jit(solution)/shard_map/all_gather | solution.py:38
  242.5 3.2 convolution_subtract_fusion.2
  245.6 0.0 copy-start
  245.7 1.3 copy-done
  247.0 4.7 %fusion.4 = f32[256,512]{0,1:T(8,128)S(1)} fusion(f32[1024,512]{1,0:T(8,128)S(1)} %convolution_subtract_fusion.2, f32[1024,1024]{1,0:T(8,128)} %reshape_reshape.6), kind=kOutput, calls=%fused_computation.8 | convolution fusion | flops 1610612736 | bytes 3670016 | tf_op jit(solution)/shard_map/dot_general | solution.py:50
  251.7 24.1 %all_to_all.21 = f32[16,256,32]{1,2,0:T(8,128)S(1)} all-to-all(f32[16,256,32]{1,2,0:T(8,128)S(1)} %bitcast.31), channel_id=1, replica_groups=mesh['row'=16,'col'=32] {'row'}, dimensions={0} | all-to-all | bytes 1048576 | tf_op jit(solution)/shard_map/all_to_all | solution.py:14
  275.8 0.3 fusion.14
  276.2 34.4 %all_gather.22 = f32[256,512]{0,1:T(8,128)S(1)} all-gather(f32[256,32]{0,1:T(8,128)S(1)} %fusion.14), channel_id=1, replica_groups=mesh['row'=16,'col'=32] {'row'}, dimensions={1}, use_global_device_ids=true | all-gather | bytes 557056 | tf_op jit(solution)/shard_map/all_gather | solution.py:38
  310.6 3.8 convolution_subtract_fusion.1
  314.3 4.7 %fusion.1 = f32[256,512]{0,1:T(8,128)S(1)} fusion(f32[1024,512]{1,0:T(8,128)S(1)} %convolution_subtract_fusion.1, f32[1024,1024]{1,0:T(8,128)} %reshape_reshape.6), kind=kOutput, calls=%fused_computation.5 | convolution fusion | flops 1610612736 | bytes 3670016 | tf_op jit(solution)/shard_map/dot_general | solution.py:50
  319.0 23.3 %all_to_all.22 = f32[16,256,32]{1,2,0:T(8,128)} all-to-all(f32[16,256,32]{1,2,0:T(8,128)S(1)} %bitcast.32), channel_id=1, replica_groups=mesh['row'=16,'col'=32] {'row'}, dimensions={0} | all-to-all | bytes 1048576 | tf_op jit(solution)/shard_map/all_to_all | solution.py:14
  342.3 1.1 reduce_sum.39
  343.4 0.3 fusion.12
  343.7 34.4 %all_gather.23 = f32[256,512]{0,1:T(8,128)S(1)} all-gather(f32[256,32]{0,1:T(8,128)S(1)} %fusion.12), channel_id=1, replica_groups=mesh['row'=16,'col'=32] {'row'}, dimensions={1}, use_global_device_ids=true | all-gather | bytes 557056 | tf_op jit(solution)/shard_map/all_gather | solution.py:38
  378.1 4.4 %convolution_subtract_fusion = f32[1024,512]{1,0:T(8,128)} fusion(f32[1024,512]{1,0:T(8,128)S(1)} %convolution_subtract_fusion.1, f32[256,512]{0,1:T(8,128)S(1)} %all_gather.23, f32[1024,1024]{1,0:T(8,128)} %reshape_reshape.6), kind=kOutput, calls=%fused_computation | convolution fusion | flops 1611137024 | bytes 5767168 | tf_op jit(solution)/shard_map/dot_general | solution.py:52
  (2 shorter events, 0.1 us)
Async XLA Ops:
  6.5 70.4 %all-gather.3.cloned.1.call-start = ((), (), s32[]{:S(2)}) async-start(), calls=%async_computation.4 | async-start | bytes 5406720 | tf_op jit(solution)/shard_map/all_gather | solution.py:26
  87.1 5.2 %copy-start.1 = (f32[1024,512]{1,0:T(8,128)S(1)}, f32[1024,512]{1,0:T(8,128)}, u32[]{:S(2)}) copy-start(f32[1024,512]{1,0:T(8,128)} %param.3) | copy-start | bytes 6291460
  97.7 12.4 %slice-start = ((f32[32,40960]{1,0:T(8,128)}), f32[32,8192]{1,0:T(8,128)S(1)}, s32[]{:S(2)}) async-start(f32[32,40960]{1,0:T(8,128)} %reshape.24), calls=%async_computation.5 | async-start | bytes 2097152 | tf_op jit(solution)/shard_map/slice | solution.py:28
  97.7 41.7 %all-to-all-start = ((f32[16,256,32]{1,2,0:T(8,128)}), f32[16,256,32]{1,2,0:T(8,128)S(1)}, u32[]{:S(2)}, u32[]{:S(2)}) async-start(f32[16,256,32]{1,2,0:T(8,128)} %bitcast.1), calls=%async_computation | async-start | bytes 1048576 | tf_op jit(solution)/shard_map/all_to_all | solution.py:14
  245.6 1.3 copy-start
Sparse Core Ops, SparseCore 0:
  10.5 66.4 all-gather.2
where the time goes:
time: 390 us; the launch traced here: 389 us
  blocking collectives  209 us (54%)
  waiting for transfers between devices  97 us (25%)
  matrix products  36 us (9%)
  local copies, waits for them, and re-layouts  18.5 us (5%)
  between operations  13.5 us (3%)
  starting transfers between devices  12.4 us (3%)
    all_gather x4, blocking collectives, settle(): return lax.all_gather(local_applied, 'row', axis=1, tiled=True)  136 us
    all_to_all x3, blocking collectives, summed_on_arrival(): lax.all_to_all(parts, axis, split_axis=0, concat_axis=0, tiled=True)  73.3 us
    all_gather x1, waiting for transfers between devices, gather_together(): lines, at, gathered = (lax.all_gather(line, axis), 0, [])  68 us
    all_to_all x1, waiting for transfers between devices, summed_on_arrival(): lax.all_to_all(parts, axis, split_axis=0, concat_axis=0, tiled=True)  29 us
    dot_general x4, matrix products, per_device(): partial_value = jnp.dot(vblock.T, current, precision=exact)  19.5 us
    dot_general x4, matrix products, per_device(): current = current - jnp.dot(vblock, applied, precision=exact)  15.1 us
    all_to_all x1, starting transfers between devices, summed_on_arrival(): lax.all_to_all(parts, axis, split_axis=0, concat_axis=0, tiled=True)  12.4 us
  transfers between devices with their start and end apart: 2, of which 2 were waited for; matrix products, arithmetic and copies ran while one was open for 0% of the time, Pallas kernels for 0%

commit v1 on v0

v1 whole, which is shorter than its diff:
```python
import jax
import jax.numpy as jnp
from jax import lax
from jax.sharding import PartitionSpec as P

HIGH = lax.Precision.HIGH
EXACT = lax.Precision.HIGHEST


def exchange_hops(ranks):
    hops, at = [], 1
    count = ranks.bit_length() - 1
    for step in range(count):
        hops.append(at)
        at += (-2) ** (step + 1)
    return hops


def block_order(ranks):
    hops = exchange_hops(ranks)

    def kept(rank, step):
        if step == len(hops):
            return [rank]
        hop = hops[step] if rank % 2 == 0 else -hops[step]
        return kept((rank + hop) % ranks, step + 1) + kept(rank, step + 1)

    return kept(0, 0)


def partners(rows, cols, hop):
    pairs = []
    for row in range(rows):
        for col in range(cols):
            sign = 1 if (row + col) % 2 == 0 else -1
            pairs.append((row * cols + col, (row + sign * hop) % rows * cols + col))
    return pairs


class Rows:
    def __init__(self, rows, cols):
        self.rows, self.cols = rows, cols
        self.pairs = [partners(rows, cols, hop) for hop in exchange_hops(rows)]
        order = block_order(rows)
        place = [order.index(block) for block in range(rows)]
        row, col = lax.axis_index("row"), lax.axis_index("col")
        sign = jnp.where((row + col) % 2 == 0, 1, -1)
        self.order = (row + sign * jnp.array(order, jnp.int32)) % rows
        self.place = jnp.array(place, jnp.int32)[sign * (jnp.arange(rows, dtype=jnp.int32) - row) % rows]

    def scattered(self, array):
        held = array.reshape(self.rows, -1, array.shape[1])[self.order]
        for pairs in self.pairs:
            half = held.shape[0] // 2
            held = held[half:] + lax.ppermute(held[:half], ("row", "col"), pairs)
        return held[0]

    def gathered(self, array):
        held = array[None]
        for pairs in reversed(self.pairs):
            held = jnp.concatenate([lax.ppermute(held, ("row", "col"), pairs), held])
        return held[self.place].reshape(-1, array.shape[1])


def gathered_halves(array, cols):
    height, width = array.shape
    halves = jnp.moveaxis(array.reshape(height, 2, width // 2), 1, 0)
    sent = jnp.broadcast_to(halves[None], (cols // 2, 2, height, width // 2)).reshape(cols, height, width // 2)
    own = lax.all_to_all(sent, "col", 0, 0, tiled=True).reshape(cols * height, width // 2)
    return own, lax.ppermute(own, "col", [(i, i ^ 1) for i in range(cols)])


def summed_over_rows(array, rows):
    height, width = array.shape
    tiles = -(-width // (128 * rows)) * rows
    padded = jnp.pad(array, ((0, 0), (0, tiles * 128 - width)))
    parts = jnp.moveaxis(padded.reshape(height, rows, -1), 1, 0)
    part = lax.all_to_all(parts, "row", 0, 0, tiled=True).sum(axis=0)
    sent = jnp.broadcast_to(part[None], parts.shape)
    whole = lax.all_to_all(sent, "row", 0, 0, tiled=True)
    return jnp.moveaxis(whole, 0, 1).reshape(height, -1)[:, :width]


def per_device(weight_basis, panels, factors):
    rows, cols = lax.axis_size("row"), lax.axis_size("col")
    over_rows = Rows(rows, cols)
    width = panels.shape[1]
    half = width // 2
    slab, block = factors.shape[0], factors.shape[0] * cols
    blocks = width // block
    col = lax.axis_index("col")
    first = col % 2 == 0

    def natural(own, other):
        return jnp.where(first, own, other), jnp.where(first, other, own)

    own, other = gathered_halves(panels, cols)

    def projected(v):
        w = lax.dot_general(weight_basis, v, (((0,), (0,)), ((), ())), precision=HIGH)
        return over_rows.scattered(w)

    w_own, w_other = projected(own), projected(other)

    picked = []
    for j in range(1, blocks):
        at = j * block % half + col * slab
        is_own = first == (j * block < half)
        a = lax.dynamic_slice(own, (0, at), (own.shape[0], slab))
        b = lax.dynamic_slice(other, (0, at), (own.shape[0], slab))
        picked.append(jnp.where(is_own, a, b))
    picked = jnp.concatenate(picked, axis=1)
    over = (((0,), (0,)), ((), ()))
    gram = jnp.concatenate(
        natural(
            lax.dot_general(picked, own, over, precision=EXACT),
            lax.dot_general(picked, other, over, precision=EXACT),
        ),
        axis=1,
    )
    gram = [gram[(j - 1) * slab : j * slab, : j * block] for j in range(1, blocks)]
    gram = summed_over_rows(jnp.concatenate(gram, axis=1), rows)
    small = jnp.concatenate(natural(*gathered_halves(jnp.concatenate([gram, factors], axis=1), cols)), axis=1)

    left = jnp.concatenate(natural(w_own, w_other), axis=1)
    applied, at = [], small.shape[1]
    for j in reversed(range(blocks)):
        triangle = small[:, at - block : at]
        at -= block
        applied.insert(
            0,
            lax.dot_general(left[:, j * block :], triangle, (((1,), (1,)), ((), ())), precision=EXACT),
        )
        if j:
            start = block * (j * (j - 1) // 2)
            cross = small[:, start : start + j * block]
            left = left[:, : j * block] - jnp.dot(applied[0], cross, precision=EXACT)
    applied = jnp.concatenate(applied, axis=1)
    y_own, y_other = natural(applied[:, :half], applied[:, half:])

    current = weight_basis
    for v, y in ((own, y_own), (other, y_other)):
        y = over_rows.gathered(y)
        current = current - lax.dot_general(v, y, (((1,), (1,)), ((), ())), precision=HIGH)
    return current


def solution(mesh):
    placed = (P("row", "col"), P(("row", "col"), None), P("col", None))
    return jax.shard_map(
        per_device, mesh=mesh, in_specs=placed, out_specs=P("row", "col"), check_vma=False
    )
```

time: 390 us -> 260 us (0.67)
  blocking collectives: 209 us -> 61.5 us
  starting transfers between devices: 12.4 us -> 76.4 us
  waiting for transfers between devices: 97 us -> 54.6 us
  local copies, waits for them, and re-layouts: 18.5 us -> 33.4 us
  between operations: 13.5 us -> 0.64 us
  matrix products: 36 us -> 24.5 us
  other arithmetic: 2.9 us -> 7.5 us
    all_gather x4 -> x0, blocking collectives: 136 us -> none  [settle(): return lax.all_gather(local_applied, 'row', axis=1, tiled=True)]
    all_gather x1 -> x0, waiting for transfers between devices: 68 us -> none  [gather_together(): lines, at, gathered = (lax.all_gather(line, axis), 0, [])]
    ppermute x0 -> x18, starting transfers between devices: none -> 67.6 us  [the longest x8 32.6 us: gathered(): held = jnp.concatenate([lax.ppermute(held, ('row', 'col'), pairs), held])]
    ppermute x0 -> x18, waiting for transfers between devices: none -> 41.9 us  [the longest x8 23.4 us: gathered(): held = jnp.concatenate([lax.ppermute(held, ('row', 'col'), pairs), held])]
    all_to_all x1 -> x2, waiting for transfers between devices: 29 us -> 12.7 us  [the longest x1 12.7 us: summed_over_rows(): whole = lax.all_to_all(sent, 'row', 0, 0, tiled=True)]
    all_to_all x3 -> x2, blocking collectives: 73.3 us -> 61.5 us  [the longest x1 34.4 us: gathered_halves(): lax.all_to_all(sent, 'col', 0, 0, tiled=True)]
    dot_general x12 -> x13, matrix products: 36 us -> 24.5 us  [the longest x2 9.43 us: projected(): lax.dot_general(weight_basis, v, (((0,), (0,)), ((), ())), precision=HIGH)]
    gather x0 -> x5, local copies, waits for them, and re-layouts: none -> 9.97 us  [the longest x2 5.64 us: scattered(): held = array.reshape(self.rows, -1, array.shape[1])[self.order]]
  transfers between devices with their start and end apart: 2 -> 20, of which waited for: 2 -> 11; matrix products, arithmetic and copies ran while one was open for 0% -> 14% of each run, Pallas kernels for 0% -> 0%
where the time goes in v1:
time: 260 us; the launch traced here: 259 us
  starting transfers between devices  76.4 us (29%)
  blocking collectives  61.5 us (24%)
  waiting for transfers between devices  54.6 us (21%)
  local copies, waits for them, and re-layouts  33.4 us (13%)
  matrix products  24.5 us (9%)
  other arithmetic  7.5 us (3%)
    all_to_all x1, blocking collectives, gathered_halves(): lax.all_to_all(sent, 'col', 0, 0, tiled=True)  34.4 us
    ppermute x8, starting transfers between devices, gathered(): held = jnp.concatenate([lax.ppermute(held, ('row', 'col'), pairs), held])  32.6 us
    ppermute x8, starting transfers between devices, scattered(): held = held[half:] + lax.ppermute(held[:half], ('row', 'col'), pairs)  29.7 us
    all_to_all x1, blocking collectives, summed_over_rows(): part = lax.all_to_all(parts, 'row', 0, 0, tiled=True).sum(axis=0)  27.1 us
    ppermute x8, waiting for transfers between devices, gathered(): held = jnp.concatenate([lax.ppermute(held, ('row', 'col'), pairs), held])  23.4 us
    ppermute x8, waiting for transfers between devices, scattered(): held = held[half:] + lax.ppermute(held[:half], ('row', 'col'), pairs)  14.6 us
    all_to_all x1, waiting for transfers between devices, summed_over_rows(): whole = lax.all_to_all(sent, 'row', 0, 0, tiled=True)  12.7 us
    unnamed x25, local copies, waits for them, and re-layouts  10 us
  transfers between devices with their start and end apart: 20, of which 11 were waited for; matrix products, arithmetic and copies ran while one was open for 14% of the time, Pallas kernels for 0%

profile of v1, /device:TPU:6, one launch (start us, length us, event | category | flops | bytes accessed | tf_op | source)
XLA Modules:
  0.0 258.5 jit_solution(10839625255123924353)
XLA Ops:
  0.0 1.0 reshape.217
  1.3 34.4 %all_to_all.20 = f32[32,32,512]{2,1,0:T(8,128)S(1)} all-to-all(f32[32,32,512]{2,1,0:T(8,128)S(1)} %bitcast.65), channel_id=1, replica_groups=mesh['row'=16,'col'=32] {'col'}, dimensions={0} | all-to-all | bytes 4194304 | tf_op jit(solution)/shard_map/all_to_all | solution.py:69
  35.8 3.3 %collective-permute-start.4 = (f32[1024,512]{1,0:T(8,128)S(1)}, f32[1024,512]{1,0:T(8,128)}, u32[]{:S(2)}, u32[]{:S(2)}) collective-permute-start(f32[1024,512]{1,0:T(8,128)S(1)} %bitcast.59), channel_id=1, source_target_pairs={{0,1},{1,0},{2,3},{3,2},{4,5},{5,4},{6,7},{7,6},{8,9},{9,8},{10,11... | collective-permute-start | bytes 6291464 | tf_op jit(solution)/shard_map/ppermute | solution.py:70
  39.1 3.9 %collective-permute-done.4 = f32[1024,512]{1,0:T(8,128)} collective-permute-done((f32[1024,512]{1,0:T(8,128)S(1)}, f32[1024,512]{1,0:T(8,128)}, u32[]{:S(2)}, u32[]{:S(2)}) %collective-permute-start.4) | collective-permute-done | bytes 2097184 | tf_op jit(solution)/shard_map/ppermute | solution.py:70
  42.9 2.6 %dynamic-slice_select_fusion.2 = (f32[1024,8]{1,0:T(8,128)S(1)}, f32[1024,8]{1,0:T(8,128)}, f32[1024,8]{1,0:T(8,128)S(1)}) fusion(f32[1024,512]{1,0:T(8,128)} %collective-permute-done.4, s32[]{:T(128)S(6)} %select_n.162, f32[1024,512]{1,0:T(8,128)S(1)} %bitcast.60, pred[]{:T(512)S(6)} %eq.16, pred[]{:T(512)S(6)} %eq.18, s32[]{:T(128)S(6)} %select_n.165), kind=kLoop, calls=%fused_computation.21 | loop fusion | flops 24576 | bytes 229386 | tf_op jit(solution)/shard_map/jit(_where)/select_n | solution.py:111
  45.5 1.2 copy.18
  47.1 2.7 %fusion.13 = f32[24,512]{1,0:T(8,128)S(1)} fusion(f32[1024,512]{1,0:T(8,128)} %collective-permute-done.4, f32[1024,8]{0,1:T(8,128)S(1)} %copy.18, f32[1024,8]{0,1:T(8,128)S(1)} %copy.17, f32[1024,8]{0,1:T(8,128)S(1)} %copy.16), kind=kOutput, calls=%fused_computation.43 | convolution fusion | flops 151044096 | bytes 2244608 | tf_op jit(solution)/shard_map/dot_general | solution.py:117
  49.8 1.1 broadcast_select_fusion.3
  51.0 27.1 %all_to_all.21 = f32[16,8,128]{2,1,0:T(8,128)S(1)} all-to-all(f32[16,8,128]{2,1,0:T(8,128)S(1)} %fusion.16), channel_id=1, replica_groups=mesh['row'=16,'col'=32] {'row'}, dimensions={0} | all-to-all | bytes 131072 | tf_op jit(solution)/shard_map/all_to_all | solution.py:78
  78.1 0.6 broadcast_in_dim.10
  78.7 3.5 %all-to-all-start.2 = ((f32[16,8,128]{2,1,0:T(8,128)}), f32[16,8,128]{2,1,0:T(8,128)S(1)}, u32[]{:S(2)}, u32[]{:S(2)}) async-start(f32[16,8,128]{2,1,0:T(8,128)} %broadcast_in_dim.10), calls=%async_computation.2 | async-start | bytes 131072 | tf_op jit(solution)/shard_map/all_to_all | solution.py:80
  82.3 12.7 %all-to-all-done.2 = f32[16,8,128]{2,1,0:T(8,128)S(1)} async-done(((f32[16,8,128]{2,1,0:T(8,128)}), f32[16,8,128]{2,1,0:T(8,128)S(1)}, u32[]{:S(2)}, u32[]{:S(2)}) %all-to-all-start.2) | async-done | bytes 65568 | tf_op jit(solution)/shard_map/all_to_all | solution.py:80
  95.0 1.2 broadcast_in_dim.11
  96.2 5.3 %all-to-all-start.3 = ((f32[32,8,1280]{2,1,0:T(8,128)}), f32[32,8,1280]{2,1,0:T(8,128)S(1)}, u32[]{:S(2)}, u32[]{:S(2)}) async-start(f32[32,8,1280]{2,1,0:T(8,128)} %bitcast.15), calls=%async_computation.3 | async-start | bytes 2621440 | tf_op jit(solution)/shard_map/all_to_all | solution.py:69
  101.5 2.9 %copy.19 = f32[1024,512]{0,1:T(8,128)} copy(f32[1024,512]{1,0:T(8,128)} %param.5) | data formatting | bytes 4194304 | tf_op args[0]
  104.4 4.4 %fusion.29 = f32[16,32,512]{2,1,0:T(8,128)} fusion(f32[16,32,1024]{2,1,0:T(8,128)} %bitcast.64, f32[1024,512,1]{1,0,2:T(8,128)S(1)} %bitcast.62), kind=kOutput, calls=%fused_computation.93 | convolution fusion | flops 1610612736 | bytes 5242880 | tf_op jit(solution)/shard_map/dot_general | solution.py:100
  108.8 2.8 %gather_fusion = f32[16,32,512]{2,1,0:T(8,128)} fusion(f32[16,32,512]{2,1,0:T(8,128)} %fusion.29, s32[1024]{0:T(1024)S(1)} %pad_clamp_fusion.2), kind=kCustom, calls=%fused_computation | custom fusion | bytes 2097216 | tf_op jit(solution)/shard_map/gather | solution.py:52
  111.6 1.9 slice.147
  113.5 2.9 %collective-permute-start = (f32[8,32,512]{2,1,0:T(8,128)}, f32[8,32,512]{2,1,0:T(8,128)}, u32[]{:S(2)}, u32[]{:S(2)}) collective-permute-start(f32[8,32,512]{2,1,0:T(8,128)} %slice.147), channel_id=1, source_target_pairs={{0,32},{1,481},{2,34},{3,483},{4,36},{5,485},{6,38},{7,487},{8,40}... | collective-permute-start | bytes 1572872 | tf_op jit(solution)/shard_map/ppermute | solution.py:55
  116.4 5.0 %fusion.30 = f32[512,512]{1,0:T(8,128)} fusion(f32[1024,512]{1,0:T(8,128)} %param.5, f32[1024,512]{1,0:T(8,128)} %collective-permute-done.4), kind=kOutput, calls=%fused_computation.94 | convolution fusion | flops 1610612736 | bytes 5242880 | tf_op jit(solution)/shard_map/dot_general | solution.py:100
  121.4 2.8 %gather_fusion.1 = f32[16,32,512]{2,1,0:T(8,128)} fusion(f32[16,32,512]{2,1,0:T(8,128)} %bitcast.69, s32[1024]{0:T(1024)S(1)} %pad_clamp_fusion.2), kind=kCustom, calls=%fused_computation.1 | custom fusion | bytes 2097216 | tf_op jit(solution)/shard_map/gather | solution.py:52
  124.2 1.9 slice.155
  126.1 3.0 %collective-permute-start.5 = (f32[8,32,512]{2,1,0:T(8,128)}, f32[8,32,512]{2,1,0:T(8,128)}, u32[]{:S(2)}, u32[]{:S(2)}) collective-permute-start(f32[8,32,512]{2,1,0:T(8,128)} %slice.155), channel_id=1, source_target_pairs={{0,32},{1,481},{2,34},{3,483},{4,36},{5,485},{6,38},{7,487},{8,40}... | collective-permute-start | bytes 1572872 | tf_op jit(solution)/shard_map/ppermute | solution.py:55
  129.1 1.3 slice_add_fusion.1
  130.4 0.8 slice.149
  131.3 3.3 %collective-permute-start.1 = (f32[4,32,512]{2,1,0:T(8,128)}, f32[4,32,512]{2,1,0:T(8,128)}, u32[]{:S(2)}, u32[]{:S(2)}) collective-permute-start(f32[4,32,512]{2,1,0:T(8,128)} %slice.149), channel_id=1, source_target_pairs={{0,480},{1,33},{2,482},{3,35},{4,484},{5,37},{6,486},{7,39},{8,488... | collective-permute-start | bytes 786440 | tf_op jit(solution)/shard_map/ppermute | solution.py:55
  134.6 2.1 collective-permute-start.9
  136.7 1.4 collective-permute-done.5
  138.1 1.3 slice_add_fusion
  139.4 2.7 %collective-permute-start.6 = (f32[4,32,512]{2,1,0:T(8,128)S(1)}, f32[4,32,512]{2,1,0:T(8,128)S(1)}, u32[]{:S(2)}, u32[]{:S(2)}) collective-permute-start(f32[4,32,512]{2,1,0:T(8,128)S(1)} %slice.157), channel_id=1, source_target_pairs={{0,480},{1,33},{2,482},{3,35},{4,484},{5,37},{6,486},{7,39},{8,488... | collective-permute-start | bytes 786440 | tf_op jit(solution)/shard_map/ppermute | solution.py:55
  142.1 1.0 slice_add_fusion.3
  143.1 3.1 %collective-permute-start.2 = (f32[2,32,512]{2,1,0:T(8,128)S(1)}, f32[2,32,512]{2,1,0:T(8,128)S(1)}, u32[]{:S(2)}, u32[]{:S(2)}) collective-permute-start(f32[2,32,512]{2,1,0:T(8,128)S(1)} %slice.151), channel_id=1, source_target_pairs={{0,96},{1,417},{2,98},{3,419},{4,100},{5,421},{6,102},{7,423},{8,1... | collective-permute-start | bytes 393224 | tf_op jit(solution)/shard_map/ppermute | solution.py:55
  146.2 3.8 %collective-permute-done.6 = f32[4,32,512]{2,1,0:T(8,128)S(1)} collective-permute-done((f32[4,32,512]{2,1,0:T(8,128)S(1)}, f32[4,32,512]{2,1,0:T(8,128)S(1)}, u32[]{:S(2)}, u32[]{:S(2)}) %collective-permute-start.6) | collective-permute-done | bytes 262176 | tf_op jit(solution)/shard_map/ppermute | solution.py:55
  150.1 2.7 %collective-permute-start.7 = (f32[2,32,512]{2,1,0:T(8,128)S(1)}, f32[2,32,512]{2,1,0:T(8,128)S(1)}, u32[]{:S(2)}, u32[]{:S(2)}) collective-permute-start(f32[2,32,512]{2,1,0:T(8,128)S(1)} %slice.159), channel_id=1, source_target_pairs={{0,96},{1,417},{2,98},{3,419},{4,100},{5,421},{6,102},{7,423},{8,1... | collective-permute-start | bytes 393224 | tf_op jit(solution)/shard_map/ppermute | solution.py:55
  152.9 9.2 %collective-permute-start.3 = (f32[1,32,512]{2,1,0:T(8,128)S(1)}, f32[1,32,512]{2,1,0:T(8,128)S(1)}, u32[]{:S(2)}, u32[]{:S(2)}) collective-permute-start(f32[1,32,512]{2,1,0:T(8,128)S(1)} %slice.153), channel_id=1, source_target_pairs={{0,352},{1,161},{2,354},{3,163},{4,356},{5,165},{6,358},{7,167},{8... | collective-permute-start | bytes 196616 | tf_op jit(solution)/shard_map/ppermute | solution.py:55
  162.1 2.8 %collective-permute-start.8 = (f32[1,32,512]{2,1,0:T(8,128)S(1)}, f32[1,32,512]{2,1,0:T(8,128)S(1)}, u32[]{:S(2)}, u32[]{:S(2)}) collective-permute-start(f32[1,32,512]{2,1,0:T(8,128)S(1)} %slice.161), channel_id=1, source_target_pairs={{0,352},{1,161},{2,354},{3,163},{4,356},{5,165},{6,358},{7,167},{8... | collective-permute-start | bytes 196616 | tf_op jit(solution)/shard_map/ppermute | solution.py:55
  165.0 0.8 collective-permute-done.3
  165.8 8.5 %collective-permute-done.8 = f32[1,32,512]{2,1,0:T(8,128)S(1)} collective-permute-done((f32[1,32,512]{2,1,0:T(8,128)S(1)}, f32[1,32,512]{2,1,0:T(8,128)S(1)}, u32[]{:S(2)}, u32[]{:S(2)}) %collective-permute-start.8) | collective-permute-done | bytes 65568 | tf_op jit(solution)/shard_map/ppermute | solution.py:55
  177.2 3.4 %collective-permute-start.10 = (f32[1,32,512]{2,1,0:T(8,128)S(1)}, f32[1,32,512]{2,1,0:T(8,128)S(1)}, u32[]{:S(2)}, u32[]{:S(2)}) collective-permute-start(f32[1,32,512]{2,1,0:T(8,128)S(1)} %get-tuple-element.13), channel_id=1, source_target_pairs={{0,352},{1,161},{2,354},{3,163},{4,356},{5,165},{6,358},{7,167},{8... | collective-permute-start | bytes 196616 | tf_op jit(solution)/shard_map/ppermute | solution.py:61
  180.6 8.8 %collective-permute-done.10 = f32[1,32,512]{2,1,0:T(8,128)S(1)} collective-permute-done((f32[1,32,512]{2,1,0:T(8,128)S(1)}, f32[1,32,512]{2,1,0:T(8,128)S(1)}, u32[]{:S(2)}, u32[]{:S(2)}) %collective-permute-start.10) | collective-permute-done | bytes 65568 | tf_op jit(solution)/shard_map/ppermute | solution.py:61
  189.4 3.6 %collective-permute-start.11 = (f32[2,32,512]{2,1,0:T(8,128)S(1)}, f32[2,32,512]{2,1,0:T(8,128)S(1)}, u32[]{:S(2)}, u32[]{:S(2)}) collective-permute-start(f32[2,32,512]{2,1,0:T(8,128)S(1)} %pad_maximum_fusion.6), channel_id=1, source_target_pairs={{0,96},{1,417},{2,98},{3,419},{4,100},{5,421},{6,102},{7,423},{8,1... | collective-permute-start | bytes 393224 | tf_op jit(solution)/shard_map/ppermute | solution.py:61
  193.0 5.2 %collective-permute-start.14 = (f32[1,32,512]{2,1,0:T(8,128)S(1)}, f32[1,32,512]{2,1,0:T(8,128)S(1)}, u32[]{:S(2)}, u32[]{:S(2)}) collective-permute-start(f32[1,32,512]{2,1,0:T(8,128)S(1)} %get-tuple-element.12), channel_id=1, source_target_pairs={{0,352},{1,161},{2,354},{3,163},{4,356},{5,165},{6,358},{7,167},{8... | collective-permute-start | bytes 196616 | tf_op jit(solution)/shard_map/ppermute | solution.py:61
  198.2 2.5 collective-permute-done.11
  200.7 9.2 %collective-permute-start.12 = (f32[4,32,512]{2,1,0:T(8,128)S(1)}, f32[4,32,512]{2,1,0:T(8,128)S(1)}, u32[]{:S(2)}, u32[]{:S(2)}) collective-permute-start(f32[4,32,512]{2,1,0:T(8,128)S(1)} %pad_maximum_fusion.4), channel_id=1, source_target_pairs={{0,480},{1,33},{2,482},{3,35},{4,484},{5,37},{6,486},{7,39},{8,488... | collective-permute-start | bytes 786440 | tf_op jit(solution)/shard_map/ppermute | solution.py:61
  210.0 1.9 collective-permute-start.15
  211.9 0.7 gather_fusion.2
  212.6 4.5 %collective-permute-done.12 = f32[4,32,512]{2,1,0:T(8,128)S(1)} collective-permute-done((f32[4,32,512]{2,1,0:T(8,128)S(1)}, f32[4,32,512]{2,1,0:T(8,128)S(1)}, u32[]{:S(2)}, u32[]{:S(2)}) %collective-permute-start.12) | collective-permute-done | bytes 262176 | tf_op jit(solution)/shard_map/ppermute | solution.py:61
  217.1 1.9 collective-permute-start.13
  219.1 4.7 %collective-permute-start.16 = (f32[4,32,512]{2,1,0:T(8,128)S(1)}, f32[4,32,512]{2,1,0:T(8,128)S(1)}, u32[]{:S(2)}, u32[]{:S(2)}) collective-permute-start(f32[4,32,512]{2,1,0:T(8,128)S(1)} %pad_maximum_fusion.5), channel_id=1, source_target_pairs={{0,480},{1,33},{2,482},{3,35},{4,484},{5,37},{6,486},{7,39},{8,488... | collective-permute-start | bytes 786440 | tf_op jit(solution)/shard_map/ppermute | solution.py:61
  223.8 7.6 %collective-permute-done.16 = f32[4,32,512]{2,1,0:T(8,128)S(1)} collective-permute-done((f32[4,32,512]{2,1,0:T(8,128)S(1)}, f32[4,32,512]{2,1,0:T(8,128)S(1)}, u32[]{:S(2)}, u32[]{:S(2)}) %collective-permute-start.16) | collective-permute-done | bytes 262176 | tf_op jit(solution)/shard_map/ppermute | solution.py:61
  231.4 0.9 pad_maximum_fusion.3
  232.3 2.7 %collective-permute-start.17 = (f32[8,32,512]{2,1,0:T(8,128)}, f32[8,32,512]{2,1,0:T(8,128)}, u32[]{:S(2)}, u32[]{:S(2)}) collective-permute-start(f32[8,32,512]{2,1,0:T(8,128)} %pad_maximum_fusion.3), channel_id=1, source_target_pairs={{0,32},{1,481},{2,34},{3,483},{4,36},{5,485},{6,38},{7,487},{8,40}... | collective-permute-start | bytes 1572872 | tf_op jit(solution)/shard_map/ppermute | solution.py:61
  235.0 0.9 constant_dynamic-update-slice_fusion.4
  235.8 0.7 constant_dynamic-update-slice_fusion.3
  236.6 0.7 constant_dynamic-update-slice_fusion.2
  237.3 0.6 constant_dynamic-update-slice_fusion.1
  238.5 1.8 gather_fusion.3
  240.4 3.2 %fusion.31 = f32[512,1024]{1,0:T(8,128)} fusion(f32[512,512]{1,0:T(8,128)S(1)} %bitcast.68, f32[1024,512]{1,0:T(8,128)S(1)} %bitcast.63), kind=kOutput, calls=%fused_computation.95 | convolution fusion | flops 1610612736 | bytes 5242880 | tf_op jit(solution)/shard_map/dot_general | solution.py:144
  243.7 2.0 constant_dynamic-update-slice_fusion.9
  245.7 0.7 constant_dynamic-update-slice_fusion.8
  246.4 0.7 constant_dynamic-update-slice_fusion.7
  248.4 1.8 gather_fusion.4
  250.2 5.4 %bitcast_subtract_fusion = f32[1024,512]{0,1:T(8,128)} fusion(f32[1024,512]{0,1:T(8,128)S(1)} %copy-done.1, f32[512,1024]{1,0:T(8,128)} %fusion.31, f32[512,512]{1,0:T(8,128)S(1)} %bitcast.67, f32[1024,512]{1,0:T(8,128)} %collective-permute-done.4), kind=kOutput, calls=%fused_computation.5 | convolution fusion | flops 1611661312 | bytes 9437184 | tf_op jit(solution)/shard_map/dot_general | solution.py:144
  255.7 2.9 %copy.20 = f32[1024,512]{1,0:T(8,128)} copy(f32[1024,512]{0,1:T(8,128)} %bitcast_subtract_fusion) | data formatting | bytes 4194304 | tf_op jit(solution)/shard_map/sub | solution.py:144
  (68 shorter events, 5.9 us)
Async XLA Ops:
  35.8 7.2 %collective-permute-start.4 = (f32[1024,512]{1,0:T(8,128)S(1)}, f32[1024,512]{1,0:T(8,128)}, u32[]{:S(2)}, u32[]{:S(2)}) collective-permute-start(f32[1024,512]{1,0:T(8,128)S(1)} %bitcast.59), channel_id=1, source_target_pairs={{0,1},{1,0},{2,3},{3,2},{4,5},{5,4},{6,7},{7,6},{8,9},{9,8},{10,11... | collective-permute-start | bytes 6291464 | tf_op jit(solution)/shard_map/ppermute | solution.py:70
  47.1 35.2 %copy-start.7 = (s32[16]{0:T(128)S(1)}, s32[16]{0:T(128)}, u32[]{:S(2)}) copy-start(s32[16]{0:T(128)} %constant.68.clone) | copy-start | bytes 196
  49.8 45.2 %copy-start.6 = (f32[8,1024]{1,0:T(8,128)S(1)}, f32[8,1024]{1,0:T(8,128)}, u32[]{:S(2)}) copy-start(f32[8,1024]{1,0:T(8,128)} %param.7) | copy-start | bytes 98308
  78.7 16.3 %all-to-all-start.2 = ((f32[16,8,128]{2,1,0:T(8,128)}), f32[16,8,128]{2,1,0:T(8,128)S(1)}, u32[]{:S(2)}, u32[]{:S(2)}) async-start(f32[16,8,128]{2,1,0:T(8,128)} %broadcast_in_dim.10), calls=%async_computation.2 | async-start | bytes 131072 | tf_op jit(solution)/shard_map/all_to_all | solution.py:80
  96.2 38.4 %all-to-all-start.3 = ((f32[32,8,1280]{2,1,0:T(8,128)}), f32[32,8,1280]{2,1,0:T(8,128)S(1)}, u32[]{:S(2)}, u32[]{:S(2)}) async-start(f32[32,8,1280]{2,1,0:T(8,128)} %bitcast.15), calls=%async_computation.3 | async-start | bytes 2621440 | tf_op jit(solution)/shard_map/all_to_all | solution.py:69
  113.5 15.5 %collective-permute-start = (f32[8,32,512]{2,1,0:T(8,128)}, f32[8,32,512]{2,1,0:T(8,128)}, u32[]{:S(2)}, u32[]{:S(2)}) collective-permute-start(f32[8,32,512]{2,1,0:T(8,128)} %slice.147), channel_id=1, source_target_pairs={{0,32},{1,481},{2,34},{3,483},{4,36},{5,485},{6,38},{7,487},{8,40}... | collective-permute-start | bytes 1572872 | tf_op jit(solution)/shard_map/ppermute | solution.py:55
  126.1 12.0 %collective-permute-start.5 = (f32[8,32,512]{2,1,0:T(8,128)}, f32[8,32,512]{2,1,0:T(8,128)}, u32[]{:S(2)}, u32[]{:S(2)}) collective-permute-start(f32[8,32,512]{2,1,0:T(8,128)} %slice.155), channel_id=1, source_target_pairs={{0,32},{1,481},{2,34},{3,483},{4,36},{5,485},{6,38},{7,487},{8,40}... | collective-permute-start | bytes 1572872 | tf_op jit(solution)/shard_map/ppermute | solution.py:55
  130.4 0.9 copy-start.2
  131.3 10.8 %collective-permute-start.1 = (f32[4,32,512]{2,1,0:T(8,128)}, f32[4,32,512]{2,1,0:T(8,128)}, u32[]{:S(2)}, u32[]{:S(2)}) collective-permute-start(f32[4,32,512]{2,1,0:T(8,128)} %slice.149), channel_id=1, source_target_pairs={{0,480},{1,33},{2,482},{3,35},{4,484},{5,37},{6,486},{7,39},{8,488... | collective-permute-start | bytes 786440 | tf_op jit(solution)/shard_map/ppermute | solution.py:55
  134.6 7.5 %copy-start.3 = (f32[8,32,512]{2,1,0:T(8,128)S(1)}, f32[8,32,512]{2,1,0:T(8,128)}, u32[]{:S(2)}) copy-start(f32[8,32,512]{2,1,0:T(8,128)} %copy-done.2) | copy-start | bytes 1572868
  134.6 39.7 %collective-permute-start.9 = (f32[256,1280]{1,0:T(8,128)S(1)}, f32[256,1280]{1,0:T(8,128)S(1)}, u32[]{:S(2)}, u32[]{:S(2)}) collective-permute-start(f32[256,1280]{1,0:T(8,128)S(1)} %bitcast.66), channel_id=1, source_target_pairs={{0,1},{1,0},{2,3},{3,2},{4,5},{5,4},{6,7},{7,6},{8,9},{9,8},{10,11... | collective-permute-start | bytes 3932168 | tf_op jit(solution)/shard_map/ppermute | solution.py:70
  139.4 10.6 %collective-permute-start.6 = (f32[4,32,512]{2,1,0:T(8,128)S(1)}, f32[4,32,512]{2,1,0:T(8,128)S(1)}, u32[]{:S(2)}, u32[]{:S(2)}) collective-permute-start(f32[4,32,512]{2,1,0:T(8,128)S(1)} %slice.157), channel_id=1, source_target_pairs={{0,480},{1,33},{2,482},{3,35},{4,484},{5,37},{6,486},{7,39},{8,488... | collective-permute-start | bytes 786440 | tf_op jit(solution)/shard_map/ppermute | solution.py:55
  143.1 9.7 %collective-permute-start.2 = (f32[2,32,512]{2,1,0:T(8,128)S(1)}, f32[2,32,512]{2,1,0:T(8,128)S(1)}, u32[]{:S(2)}, u32[]{:S(2)}) collective-permute-start(f32[2,32,512]{2,1,0:T(8,128)S(1)} %slice.151), channel_id=1, source_target_pairs={{0,96},{1,417},{2,98},{3,419},{4,100},{5,421},{6,102},{7,423},{8,1... | collective-permute-start | bytes 393224 | tf_op jit(solution)/shard_map/ppermute | solution.py:55
  150.1 12.0 %collective-permute-start.7 = (f32[2,32,512]{2,1,0:T(8,128)S(1)}, f32[2,32,512]{2,1,0:T(8,128)S(1)}, u32[]{:S(2)}, u32[]{:S(2)}) collective-permute-start(f32[2,32,512]{2,1,0:T(8,128)S(1)} %slice.159), channel_id=1, source_target_pairs={{0,96},{1,417},{2,98},{3,419},{4,100},{5,421},{6,102},{7,423},{8,1... | collective-permute-start | bytes 393224 | tf_op jit(solution)/shard_map/ppermute | solution.py:55
  152.9 13.0 %collective-permute-start.3 = (f32[1,32,512]{2,1,0:T(8,128)S(1)}, f32[1,32,512]{2,1,0:T(8,128)S(1)}, u32[]{:S(2)}, u32[]{:S(2)}) collective-permute-start(f32[1,32,512]{2,1,0:T(8,128)S(1)} %slice.153), channel_id=1, source_target_pairs={{0,352},{1,161},{2,354},{3,163},{4,356},{5,165},{6,358},{7,167},{8... | collective-permute-start | bytes 196616 | tf_op jit(solution)/shard_map/ppermute | solution.py:55
  162.1 12.2 %collective-permute-start.8 = (f32[1,32,512]{2,1,0:T(8,128)S(1)}, f32[1,32,512]{2,1,0:T(8,128)S(1)}, u32[]{:S(2)}, u32[]{:S(2)}) collective-permute-start(f32[1,32,512]{2,1,0:T(8,128)S(1)} %slice.161), channel_id=1, source_target_pairs={{0,352},{1,161},{2,354},{3,163},{4,356},{5,165},{6,358},{7,167},{8... | collective-permute-start | bytes 196616 | tf_op jit(solution)/shard_map/ppermute | solution.py:55
  175.5 36.5 %copy-start = (s32[16]{0:T(128)S(1)}, s32[16]{0:T(128)}, u32[]{:S(2)}) copy-start(s32[16]{0:T(128)} %constant.69.clone) | copy-start | bytes 196
  177.2 12.2 %collective-permute-start.10 = (f32[1,32,512]{2,1,0:T(8,128)S(1)}, f32[1,32,512]{2,1,0:T(8,128)S(1)}, u32[]{:S(2)}, u32[]{:S(2)}) collective-permute-start(f32[1,32,512]{2,1,0:T(8,128)S(1)} %get-tuple-element.13), channel_id=1, source_target_pairs={{0,352},{1,161},{2,354},{3,163},{4,356},{5,165},{6,358},{7,167},{8... | collective-permute-start | bytes 196616 | tf_op jit(solution)/shard_map/ppermute | solution.py:61
  189.4 11.3 %collective-permute-start.11 = (f32[2,32,512]{2,1,0:T(8,128)S(1)}, f32[2,32,512]{2,1,0:T(8,128)S(1)}, u32[]{:S(2)}, u32[]{:S(2)}) collective-permute-start(f32[2,32,512]{2,1,0:T(8,128)S(1)} %pad_maximum_fusion.6), channel_id=1, source_target_pairs={{0,96},{1,417},{2,98},{3,419},{4,100},{5,421},{6,102},{7,423},{8,1... | collective-permute-start | bytes 393224 | tf_op jit(solution)/shard_map/ppermute | solution.py:61
  193.0 17.0 %collective-permute-start.14 = (f32[1,32,512]{2,1,0:T(8,128)S(1)}, f32[1,32,512]{2,1,0:T(8,128)S(1)}, u32[]{:S(2)}, u32[]{:S(2)}) collective-permute-start(f32[1,32,512]{2,1,0:T(8,128)S(1)} %get-tuple-element.12), channel_id=1, source_target_pairs={{0,352},{1,161},{2,354},{3,163},{4,356},{5,165},{6,358},{7,167},{8... | collective-permute-start | bytes 196616 | tf_op jit(solution)/shard_map/ppermute | solution.py:61
  200.7 16.4 %collective-permute-start.12 = (f32[4,32,512]{2,1,0:T(8,128)S(1)}, f32[4,32,512]{2,1,0:T(8,128)S(1)}, u32[]{:S(2)}, u32[]{:S(2)}) collective-permute-start(f32[4,32,512]{2,1,0:T(8,128)S(1)} %pad_maximum_fusion.4), channel_id=1, source_target_pairs={{0,480},{1,33},{2,482},{3,35},{4,484},{5,37},{6,486},{7,39},{8,488... | collective-permute-start | bytes 786440 | tf_op jit(solution)/shard_map/ppermute | solution.py:61
  210.0 9.1 %collective-permute-start.15 = (f32[2,32,512]{2,1,0:T(8,128)S(1)}, f32[2,32,512]{2,1,0:T(8,128)S(1)}, u32[]{:S(2)}, u32[]{:S(2)}) collective-permute-start(f32[2,32,512]{2,1,0:T(8,128)S(1)} %pad_maximum_fusion.7), channel_id=1, source_target_pairs={{0,96},{1,417},{2,98},{3,419},{4,100},{5,421},{6,102},{7,423},{8,1... | collective-permute-start | bytes 393224 | tf_op jit(solution)/shard_map/ppermute | solution.py:61
  217.1 17.9 %collective-permute-start.13 = (f32[8,32,512]{2,1,0:T(8,128)S(1)}, f32[8,32,512]{2,1,0:T(8,128)S(1)}, u32[]{:S(2)}, u32[]{:S(2)}) collective-permute-start(f32[8,32,512]{2,1,0:T(8,128)S(1)} %pad_maximum_fusion.2), channel_id=1, source_target_pairs={{0,32},{1,481},{2,34},{3,483},{4,36},{5,485},{6,38},{7,487},{8,40}... | collective-permute-start | bytes 1572872 | tf_op jit(solution)/shard_map/ppermute | solution.py:61
  219.1 12.3 %collective-permute-start.16 = (f32[4,32,512]{2,1,0:T(8,128)S(1)}, f32[4,32,512]{2,1,0:T(8,128)S(1)}, u32[]{:S(2)}, u32[]{:S(2)}) collective-permute-start(f32[4,32,512]{2,1,0:T(8,128)S(1)} %pad_maximum_fusion.5), channel_id=1, source_target_pairs={{0,480},{1,33},{2,482},{3,35},{4,484},{5,37},{6,486},{7,39},{8,488... | collective-permute-start | bytes 786440 | tf_op jit(solution)/shard_map/ppermute | solution.py:61
  231.4 6.5 %copy-start.4 = (f32[4,32,512]{2,1,0:T(8,128)}, f32[4,32,512]{2,1,0:T(8,128)S(1)}, u32[]{:S(2)}) copy-start(f32[4,32,512]{2,1,0:T(8,128)S(1)} %collective-permute-done.16) | copy-start | bytes 786436
  232.3 11.4 %collective-permute-start.17 = (f32[8,32,512]{2,1,0:T(8,128)}, f32[8,32,512]{2,1,0:T(8,128)}, u32[]{:S(2)}, u32[]{:S(2)}) collective-permute-start(f32[8,32,512]{2,1,0:T(8,128)} %pad_maximum_fusion.3), channel_id=1, source_target_pairs={{0,32},{1,481},{2,34},{3,483},{4,36},{5,485},{6,38},{7,487},{8,40}... | collective-permute-start | bytes 1572872 | tf_op jit(solution)/shard_map/ppermute | solution.py:61
  240.4 5.3 %copy-start.5 = (f32[4,32,512]{2,1,0:T(8,128)S(1)}, f32[4,32,512]{2,1,0:T(8,128)}, u32[]{:S(2)}) copy-start(f32[4,32,512]{2,1,0:T(8,128)} %copy-done.4) | copy-start | bytes 786436
  243.5 6.7 %copy-start.1 = (f32[1024,512]{0,1:T(8,128)S(1)}, f32[1024,512]{0,1:T(8,128)}, u32[]{:S(2)}) copy-start(f32[1024,512]{0,1:T(8,128)} %copy.19) | copy-start | bytes 6291460

commit v2 on v1

--- a/solution.py
+++ b/solution.py
@@ -1,9 +1,13 @@
+import functools
+
 import jax
 import jax.numpy as jnp
 from jax import lax
+from jax.experimental import pallas as pl
+from jax.experimental.pallas import tpu as pltpu
 from jax.sharding import PartitionSpec as P
 
-HIGH = lax.Precision.HIGH
+
 EXACT = lax.Precision.HIGHEST
 
 
@@ -39,27 +43,129 @@
 
 class Rows:
     def __init__(self, rows, cols):
-        self.rows, self.cols = rows, cols
         self.pairs = [partners(rows, cols, hop) for hop in exchange_hops(rows)]
-        order = block_order(rows)
-        place = [order.index(block) for block in range(rows)]
         row, col = lax.axis_index("row"), lax.axis_index("col")
         sign = jnp.where((row + col) % 2 == 0, 1, -1)
-        self.order = (row + sign * jnp.array(order, jnp.int32)) % rows
-        self.place = jnp.array(place, jnp.int32)[sign * (jnp.arange(rows, dtype=jnp.int32) - row) % rows]
-
-    def scattered(self, array):
-        held = array.reshape(self.rows, -1, array.shape[1])[self.order]
+        self.order = (row + sign * jnp.array(block_order(rows), jnp.int32)) % rows
+
+    def scattered(self, sent, kept):
         for pairs in self.pairs:
-            half = held.shape[0] // 2
-            held = held[half:] + lax.ppermute(held[:half], ("row", "col"), pairs)
-        return held[0]
+            come = lax.ppermute(sent, ("row", "col"), pairs)
+            half = kept.shape[0] // 2
+            if half == 0:
+                return (kept + come)[0]
+            sent = kept[:half] + come[:half]
+            kept = kept[half:] + come[half:]
 
     def gathered(self, array):
         held = array[None]
         for pairs in reversed(self.pairs):
-            held = jnp.concatenate([lax.ppermute(held, ("row", "col"), pairs), held])
-        return held[self.place].reshape(-1, array.shape[1])
+            come = lax.ppermute(held, ("row", "col"), pairs)
+            if held.shape[0] * 2 == self.order.shape[0]:
+                return come, held
+            held = jnp.concatenate([come, held])
+
+
+def parts_of(x):
+    high = x.astype(jnp.bfloat16)
+    return high, (x - high.astype(jnp.float32)).astype(jnp.bfloat16)
+
+
+def product(a, b, dims):
+    total = None
+    for x, y in ((a[1], b[0]), (a[0], b[1]), (a[0], b[0])):
+        term = lax.dot_general(x, y, dims, preferred_element_type=jnp.float32)
+        total = term if total is None else total + term
+    return total
+
+
+def turned_kernel(c_ref, high_ref, low_ref):
+    high_ref[...], low_ref[...] = parts_of(c_ref[...].T)
+
+
+def turned(c):
+    height, width = c.shape
+    step = min(width, 128)
+    out = jax.ShapeDtypeStruct((width, height), jnp.bfloat16)
+    return pl.pallas_call(
+        turned_kernel,
+        grid=(width // step,),
+        in_specs=[pl.BlockSpec((height, step), lambda i: (0, i))],
+        out_specs=[pl.BlockSpec((step, height), lambda i: (i, 0))] * 2,
+        out_shape=[out, out],
+        cost_estimate=pl.CostEstimate(flops=8 * height * width, bytes_accessed=8 * height * width, transcendentals=0),
+        name="turned",
+    )(c)
+
+
+def projection_kernel(step, order_ref, high_ref, low_ref, v_ref, sent_ref, kept_ref, w_ref, vhigh_ref, vlow_ref):
+    vhigh_ref[...], vlow_ref[...] = parts_of(v_ref[...])
+    v = vhigh_ref[...], vlow_ref[...]
+
+    @pl.loop(0, w_ref.shape[0] // step)
+    def _(i):
+        at = pl.ds(pl.multiple_of(i * step, step), step)
+        w_ref[at, :] = product((high_ref[at, :], low_ref[at, :]), v, (((1,), (0,)), ((), ())))
+
+    half, size, _ = sent_ref.shape
+    for i in range(2 * half):
+        at = pl.ds(pl.multiple_of(order_ref[i] * size, size), size)
+        if i < half:
+            sent_ref[i] = w_ref[at, :]
+        else:
+            kept_ref[i - half] = w_ref[at, :]
+
+
+def projection(order, c_parts, v):
+    width, height = c_parts[0].shape
+    ranks, rest = order.shape[0], v.shape[1]
+    out = jax.ShapeDtypeStruct((ranks // 2, width // ranks, rest), jnp.float32)
+    whole = pl.BlockSpec(memory_space=pltpu.VMEM)
+    return pl.pallas_call(
+        functools.partial(projection_kernel, min(width, 128)),
+        in_specs=[pl.BlockSpec(memory_space=pltpu.SMEM), whole, whole, whole],
+        out_specs=[whole, whole],
+        out_shape=[out, out],
+        scratch_shapes=[
+            pltpu.VMEM((width, rest), jnp.float32),
+            pltpu.VMEM((height, rest), jnp.bfloat16),
+            pltpu.VMEM((height, rest), jnp.bfloat16),
+        ],
+        cost_estimate=pl.CostEstimate(
+            flops=6 * width * height * rest, bytes_accessed=4 * (2 * width * rest + height * (width + rest)), transcendentals=0
+        ),
+        name="projection",
+    )(order, *c_parts, v)
+
+
+def update_kernel(step, order_ref, c_ref, v_ref, come_ref, held_ref, out_ref, high_ref, low_ref):
+    half, size, _ = come_ref.shape
+    for i in range(2 * half):
+        at = pl.ds(pl.multiple_of(order_ref[i] * size, size), size)
+        high_ref[at, :], low_ref[at, :] = parts_of(come_ref[i] if i < half else held_ref[i - half])
+    y = high_ref[...], low_ref[...]
+
+    @pl.loop(0, c_ref.shape[0] // step)
+    def _(i):
+        at = pl.ds(pl.multiple_of(i * step, step), step)
+        out_ref[at, :] = c_ref[at, :] - product(parts_of(v_ref[at, :]), y, (((1,), (1,)), ((), ())))
+
+
+def updated(order, c, v, come, held):
+    height, width = c.shape
+    rest = v.shape[1]
+    whole = pl.BlockSpec(memory_space=pltpu.VMEM)
+    return pl.pallas_call(
+        functools.partial(update_kernel, min(height, 128)),
+        in_specs=[pl.BlockSpec(memory_space=pltpu.SMEM), whole, whole, whole, whole],
+        out_specs=whole,
+        out_shape=jax.ShapeDtypeStruct((height, width), jnp.float32),
+        scratch_shapes=[pltpu.VMEM((width, rest), jnp.bfloat16)] * 2,
+        cost_estimate=pl.CostEstimate(
+            flops=6 * width * height * rest, bytes_accessed=4 * (width * rest + height * (2 * width + rest)), transcendentals=0
+        ),
+        name="updated",
+    )(order, c, v, come, held)
 
 
 def gathered_halves(array, cols):
@@ -75,8 +181,8 @@
     tiles = -(-width // (128 * rows)) * rows
     padded = jnp.pad(array, ((0, 0), (0, tiles * 128 - width)))
     parts = jnp.moveaxis(padded.reshape(height, rows, -1), 1, 0)
-    part = lax.all_to_all(parts, "row", 0, 0, tiled=True).sum(axis=0)
-    sent = jnp.broadcast_to(part[None], parts.shape)
+    part = lax.all_to_all(parts, "row", 0, 0, tiled=True)
+    sent = jnp.broadcast_to(part.sum(axis=0)[None], parts.shape)
     whole = lax.all_to_all(sent, "row", 0, 0, tiled=True)
     return jnp.moveaxis(whole, 0, 1).reshape(height, -1)[:, :width]
 
@@ -96,11 +202,11 @@
 
     own, other = gathered_halves(panels, cols)
 
-    def projected(v):
-        w = lax.dot_general(weight_basis, v, (((0,), (0,)), ((), ())), precision=HIGH)
-        return over_rows.scattered(w)
-
-    w_own, w_other = projected(own), projected(other)
+    c_parts = turned(weight_basis)
+    partial_own = projection(over_rows.order, c_parts, own)
+    partial_other = projection(over_rows.order, c_parts, other)
+    w_own = over_rows.scattered(*partial_own)
+    w_other = over_rows.scattered(*partial_other)
 
     picked = []
     for j in range(1, blocks):
@@ -140,13 +246,10 @@
 
     current = weight_basis
     for v, y in ((own, y_own), (other, y_other)):
-        y = over_rows.gathered(y)
-        current = current - lax.dot_general(v, y, (((1,), (1,)), ((), ())), precision=HIGH)
+        current = updated(over_rows.order, current, v, *over_rows.gathered(y))
     return current
 
 
 def solution(mesh):
     placed = (P("row", "col"), P(("row", "col"), None), P("col", None))
-    return jax.shard_map(
-        per_device, mesh=mesh, in_specs=placed, out_specs=P("row", "col"), check_vma=False
-    )
+    return jax.shard_map(per_device, mesh=mesh, in_specs=placed, out_specs=P("row", "col"), check_vma=False)

time: 260 us -> 243 us (0.935)
  Pallas kernels: 0 us -> 34.4 us
  local copies, waits for them, and re-layouts: 33.4 us -> 5.66 us
  matrix products: 24.5 us -> 6.4 us
  blocking collectives: 61.5 us -> 77 us
  waiting for transfers between devices: 54.6 us -> 39.4 us
  starting transfers between devices: 76.4 us -> 73.4 us
  other arithmetic: 7.5 us -> 4.79 us
    pallas_call x0 -> x5, Pallas kernels: none -> 34.4 us  [the longest x2 18.3 us: updated(): pl.pallas_call(functools.partial(update_kernel, min(height, 128)), in_spe...]
    dot_general x4 -> x0, matrix products: 18 us -> none  [the longest x2 9.43 us: projected(): lax.dot_general(weight_basis, v, (((0,), (0,)), ((), ())), precision=HIGH)]
    all_to_all x1 -> x2, blocking collectives: 27.1 us -> 42.5 us  [the longest x1 27.1 us: summed_over_rows(): part = lax.all_to_all(parts, 'row', 0, 0, tiled=True)]
    all_to_all x1 -> x0, waiting for transfers between devices: 12.7 us -> none  [summed_over_rows(): whole = lax.all_to_all(sent, 'row', 0, 0, tiled=True)]
    gather x5 -> x0, local copies, waits for them, and re-layouts: 9.97 us -> none  [the longest x2 5.64 us: scattered(): held = array.reshape(self.rows, -1, array.shape[1])[self.order]]
    unnamed x25 -> x18, local copies, waits for them, and re-layouts: 10 us -> 1.63 us
    slice x8 -> x0, local copies, waits for them, and re-layouts: 4.59 us -> none  [scattered(): held = held[half:] + lax.ppermute(held[:half], ('row', 'col'), pairs)]
    all_to_all x1 -> x0, starting transfers between devices: 3.5 us -> none  [summed_over_rows(): whole = lax.all_to_all(sent, 'row', 0, 0, tiled=True)]
  transfers between devices with their start and end apart: 20 -> 19, of which waited for: 11 -> 12; matrix products, arithmetic and copies ran while one was open for 14% -> 1% of each run, Pallas kernels for 0% -> 10%
where the time goes in v2:
time: 243 us; the launch traced here: 242 us
  blocking collectives  77 us (32%)
  starting transfers between devices  73.4 us (30%)
  waiting for transfers between devices  39.4 us (16%)
  Pallas kernels  34.4 us (14%)
  matrix products  6.4 us (3%)
  local copies, waits for them, and re-layouts  5.66 us (2%)
  other arithmetic  4.79 us (2%)
    all_to_all x1, blocking collectives, gathered_halves(): lax.all_to_all(sent, 'col', 0, 0, tiled=True)  34.4 us
    ppermute x8, starting transfers between devices, scattered(): come = lax.ppermute(sent, ('row', 'col'), pairs)  33.8 us
    ppermute x8, starting transfers between devices, gathered(): come = lax.ppermute(held, ('row', 'col'), pairs)  29.1 us
    all_to_all x1, blocking collectives, summed_over_rows(): part = lax.all_to_all(parts, 'row', 0, 0, tiled=True)  27.1 us
    ppermute x8, waiting for transfers between devices, gathered(): come = lax.ppermute(held, ('row', 'col'), pairs)  21.6 us
    pallas_call x2, Pallas kernels, updated(): pl.pallas_call(functools.partial(update_kernel, min(height, 128)), in_spe...  18.3 us
    all_to_all x1, blocking collectives, summed_over_rows(): whole = lax.all_to_all(sent, 'row', 0, 0, tiled=True)  15.5 us
    ppermute x8, waiting for transfers between devices, scattered(): come = lax.ppermute(sent, ('row', 'col'), pairs)  13.9 us
  transfers between devices with their start and end apart: 19, of which 12 were waited for; matrix products, arithmetic and copies ran while one was open for 1% of the time, Pallas kernels for 10%

profile of v2, /device:TPU:6, one launch (start us, length us, event | category | flops | bytes accessed | tf_op | source)
XLA Modules:
  0.0 241.5 jit_solution(8661463971937539984)
XLA Ops:
  0.0 1.0 reshape.141
  1.1 0.2 broadcast_in_dim.6
  1.3 34.4 %all_to_all.20 = f32[32,32,512]{2,1,0:T(8,128)S(1)} all-to-all(f32[32,32,512]{2,1,0:T(8,128)S(1)} %bitcast.36), channel_id=1, replica_groups=mesh['row'=16,'col'=32] {'col'}, dimensions={0} | all-to-all | bytes 4194304 | tf_op jit(solution)/shard_map/all_to_all | solution.py:175
  35.8 3.3 %collective-permute-start.4 = (f32[1024,512]{1,0:T(8,128)S(1)}, f32[1024,512]{1,0:T(8,128)}, u32[]{:S(2)}, u32[]{:S(2)}) collective-permute-start(f32[1024,512]{1,0:T(8,128)S(1)} %bitcast.31), channel_id=1, source_target_pairs={{0,1},{1,0},{2,3},{3,2},{4,5},{5,4},{6,7},{7,6},{8,9},{9,8},{10,11... | collective-permute-start | bytes 6291464 | tf_op jit(solution)/shard_map/ppermute | solution.py:176
  39.1 3.9 %collective-permute-done.4.v_ref = f32[1024,512]{1,0:T(8,128)} collective-permute-done((f32[1024,512]{1,0:T(8,128)S(1)}, f32[1024,512]{1,0:T(8,128)}, u32[]{:S(2)}, u32[]{:S(2)}) %collective-permute-start.4) | collective-permute-done | bytes 2097184 | tf_op jit(solution)/shard_map/ppermute | solution.py:176
  42.9 2.6 %dynamic-slice_select_fusion.2 = (f32[1024,8]{1,0:T(8,128)}, f32[1024,8]{1,0:T(8,128)S(1)}, f32[1024,8]{1,0:T(8,128)S(1)}) fusion(f32[1024,512]{1,0:T(8,128)} %collective-permute-done.4.v_ref, s32[]{:T(128)S(6)} %select_n.125, f32[1024,512]{1,0:T(8,128)S(1)} %bitcast.32, pred[]{:T(512)S(6)} %eq.16, pred[]{:T(512)S(6)} %eq.17, s32[]{:T(128)S(6)} %select_n.128), kind=kLoop, calls=%fused_computation.12 | loop fusion | flops 24576 | bytes 229386 | tf_op jit(solution)/shard_map/jit(_where)/select_n | solution.py:217
  45.6 1.2 copy.7
  46.8 0.2 copy.9
  46.9 0.2 copy.8
  47.1 2.7 %fusion.13 = f32[24,512]{1,0:T(8,128)S(1)} fusion(f32[1024,512]{1,0:T(8,128)} %collective-permute-done.4.v_ref, f32[1024,8]{0,1:T(8,128)S(1)} %copy.9, f32[1024,8]{0,1:T(8,128)S(1)} %copy.8, f32[1024,8]{0,1:T(8,128)S(1)} %copy.7), kind=kOutput, calls=%fused_computation.38 | convolution fusion | flops 151044096 | bytes 2244608 | tf_op jit(solution)/shard_map/dot_general | solution.py:223
  49.8 0.0 copy-done
  49.8 0.0 copy-start.7
  49.8 1.1 broadcast_select_fusion.3
  51.0 27.1 %all_to_all.21 = f32[16,8,128]{2,1,0:T(8,128)S(1)} all-to-all(f32[16,8,128]{2,1,0:T(8,128)S(1)} %fusion.16), channel_id=1, replica_groups=mesh['row'=16,'col'=32] {'row'}, dimensions={0} | all-to-all | bytes 131072 | tf_op jit(solution)/shard_map/all_to_all | solution.py:184
  78.1 15.5 %all_to_all.22 = f32[16,8,128]{2,1,0:T(8,128)S(1)} all-to-all(f32[16,8,128]{2,1,0:T(8,128)S(1)} %broadcast_in_dim.7), channel_id=1, replica_groups=mesh['row'=16,'col'=32] {'row'}, dimensions={0} | all-to-all | bytes 131072 | tf_op jit(solution)/shard_map/all_to_all | solution.py:186
  93.6 1.2 broadcast_in_dim.8
  94.8 5.3 %all-to-all-start.3 = ((f32[32,8,1280]{2,1,0:T(8,128)}), f32[32,8,1280]{2,1,0:T(8,128)S(1)}, u32[]{:S(2)}, u32[]{:S(2)}) async-start(f32[32,8,1280]{2,1,0:T(8,128)} %bitcast.11), calls=%async_computation.3 | async-start | bytes 2621440 | tf_op jit(solution)/shard_map/all_to_all | solution.py:175
  100.1 0.0 copy-start.8
  100.1 4.1 %turned.1 = (bf16[512,1024]{1,0:T(8,128)(2,1)}, bf16[512,1024]{1,0:T(8,128)(2,1)}) custom-call(f32[1024,512]{1,0:T(8,128)} %c_ref.3), custom_call_target="tpu_custom_call" | custom-call | flops 4194304 | bytes 4194304 | tf_op jit(solution)/shard_map/turned/pallas_call | solution.py:90
  104.2 0.5 and_select_fusion.order_ref
  104.8 5.9 %projection.2 = (f32[8,32,512]{2,1,0:T(8,128)}, f32[8,32,512]{2,1,0:T(8,128)}) custom-call(s32[16]{0:T(128)} %and_select_fusion.order_ref, bf16[512,1024]{1,0:T(8,128)(2,1)} %get-tuple-element.11.high_ref, bf16[512,1024]{1,0:T(8,128)(2,1)} %get-tuple-element.12.low_ref, f32[1024,512]{1,0:T(8,128)} %bitcast.34), custom_call_target="tpu_custom_call" | custom-call | flops 1610612736 | bytes 6291456 | tf_op jit(solution)/shard_map/projection/pallas_call | solution.py:124
  110.7 2.8 %collective-permute-start = (f32[8,32,512]{2,1,0:T(8,128)}, f32[8,32,512]{2,1,0:T(8,128)}, u32[]{:S(2)}, u32[]{:S(2)}) collective-permute-start(f32[8,32,512]{2,1,0:T(8,128)} %get-tuple-element.14), channel_id=1, source_target_pairs={{0,32},{1,481},{2,34},{3,483},{4,36},{5,485},{6,38},{7,487},{8,40}... | collective-permute-start | bytes 1572872 | tf_op jit(solution)/shard_map/ppermute | solution.py:53
  113.5 6.0 %projection.3 = (f32[8,32,512]{2,1,0:T(8,128)}, f32[8,32,512]{2,1,0:T(8,128)}) custom-call(s32[16]{0:T(128)} %and_select_fusion.order_ref, bf16[512,1024]{1,0:T(8,128)(2,1)} %get-tuple-element.11.high_ref, bf16[512,1024]{1,0:T(8,128)(2,1)} %get-tuple-element.12.low_ref, f32[1024,512]{1,0:T(8,128)} %collective-permute-done.4.v_ref), custom_call_target="tpu_custom_call" | custom-call | flops 1610612736 | bytes 6291456 | tf_op jit(solution)/shard_map/projection/pallas_call | solution.py:124
  119.5 3.3 %collective-permute-start.5 = (f32[8,32,512]{2,1,0:T(8,128)}, f32[8,32,512]{2,1,0:T(8,128)S(1)}, u32[]{:S(2)}, u32[]{:S(2)}) collective-permute-start(f32[8,32,512]{2,1,0:T(8,128)} %get-tuple-element.16), channel_id=1, source_target_pairs={{0,32},{1,481},{2,34},{3,483},{4,36},{5,485},{6,38},{7,487},{8,40}... | collective-permute-start | bytes 1572872 | tf_op jit(solution)/shard_map/ppermute | solution.py:53
  122.8 1.1 slice_add_fusion.3
  123.9 3.4 %collective-permute-start.1 = (f32[4,32,512]{2,1,0:T(8,128)S(1)}, f32[4,32,512]{2,1,0:T(8,128)S(1)}, u32[]{:S(2)}, u32[]{:S(2)}) collective-permute-start(f32[4,32,512]{2,1,0:T(8,128)S(1)} %get-tuple-element.25), channel_id=1, source_target_pairs={{0,480},{1,33},{2,482},{3,35},{4,484},{5,37},{6,486},{7,39},{8,488... | collective-permute-start | bytes 786440 | tf_op jit(solution)/shard_map/ppermute | solution.py:53
  127.4 1.9 collective-permute-start.9
  129.3 3.4 %collective-permute-done.5 = f32[8,32,512]{2,1,0:T(8,128)S(1)} collective-permute-done((f32[8,32,512]{2,1,0:T(8,128)}, f32[8,32,512]{2,1,0:T(8,128)S(1)}, u32[]{:S(2)}, u32[]{:S(2)}) %collective-permute-start.5) | collective-permute-done | bytes 524320 | tf_op jit(solution)/shard_map/ppermute | solution.py:53
  132.7 0.1 slice_add_fusion.1
  132.8 3.2 %collective-permute-start.6 = (f32[4,32,512]{2,1,0:T(8,128)S(1)}, f32[4,32,512]{2,1,0:T(8,128)S(1)}, u32[]{:S(2)}, u32[]{:S(2)}) collective-permute-start(f32[4,32,512]{2,1,0:T(8,128)S(1)} %get-tuple-element.23), channel_id=1, source_target_pairs={{0,480},{1,33},{2,482},{3,35},{4,484},{5,37},{6,486},{7,39},{8,488... | collective-permute-start | bytes 786440 | tf_op jit(solution)/shard_map/ppermute | solution.py:53
  136.0 3.0 %collective-permute-start.2 = (f32[2,32,512]{2,1,0:T(8,128)S(1)}, f32[2,32,512]{2,1,0:T(8,128)S(1)}, u32[]{:S(2)}, u32[]{:S(2)}) collective-permute-start(f32[2,32,512]{2,1,0:T(8,128)S(1)} %get-tuple-element.31), channel_id=1, source_target_pairs={{0,96},{1,417},{2,98},{3,419},{4,100},{5,421},{6,102},{7,423},{8,1... | collective-permute-start | bytes 393224 | tf_op jit(solution)/shard_map/ppermute | solution.py:53
  139.1 6.1 %collective-permute-done.6 = f32[4,32,512]{2,1,0:T(8,128)S(1)} collective-permute-done((f32[4,32,512]{2,1,0:T(8,128)S(1)}, f32[4,32,512]{2,1,0:T(8,128)S(1)}, u32[]{:S(2)}, u32[]{:S(2)}) %collective-permute-start.6) | collective-permute-done | bytes 262176 | tf_op jit(solution)/shard_map/ppermute | solution.py:53
  145.2 6.6 %collective-permute-start.7 = (f32[2,32,512]{2,1,0:T(8,128)S(1)}, f32[2,32,512]{2,1,0:T(8,128)S(1)}, u32[]{:S(2)}, u32[]{:S(2)}) collective-permute-start(f32[2,32,512]{2,1,0:T(8,128)S(1)} %get-tuple-element.29), channel_id=1, source_target_pairs={{0,96},{1,417},{2,98},{3,419},{4,100},{5,421},{6,102},{7,423},{8,1... | collective-permute-start | bytes 393224 | tf_op jit(solution)/shard_map/ppermute | solution.py:53
  151.8 3.2 %collective-permute-start.3 = (f32[1,32,512]{2,1,0:T(8,128)S(1)}, f32[1,32,512]{2,1,0:T(8,128)S(1)}, u32[]{:S(2)}, u32[]{:S(2)}) collective-permute-start(f32[1,32,512]{2,1,0:T(8,128)S(1)} %slice_add_fusion.10), channel_id=1, source_target_pairs={{0,352},{1,161},{2,354},{3,163},{4,356},{5,165},{6,358},{7,167},{8... | collective-permute-start | bytes 196616 | tf_op jit(solution)/shard_map/ppermute | solution.py:53
  155.1 0.5 collective-permute-done.7
  155.5 8.2 %collective-permute-start.8 = (f32[1,32,512]{2,1,0:T(8,128)S(1)}, f32[1,32,512]{2,1,0:T(8,128)S(1)}, u32[]{:S(2)}, u32[]{:S(2)}) collective-permute-start(f32[1,32,512]{2,1,0:T(8,128)S(1)} %slice_add_fusion.8), channel_id=1, source_target_pairs={{0,352},{1,161},{2,354},{3,163},{4,356},{5,165},{6,358},{7,167},{8... | collective-permute-start | bytes 196616 | tf_op jit(solution)/shard_map/ppermute | solution.py:53
  163.7 0.9 collective-permute-done.3
  164.7 3.0 %collective-permute-done.8 = f32[1,32,512]{2,1,0:T(8,128)S(1)} collective-permute-done((f32[1,32,512]{2,1,0:T(8,128)S(1)}, f32[1,32,512]{2,1,0:T(8,128)S(1)}, u32[]{:S(2)}, u32[]{:S(2)}) %collective-permute-start.8) | collective-permute-done | bytes 65568 | tf_op jit(solution)/shard_map/ppermute | solution.py:53
  167.7 0.2 broadcast_select_fusion
  167.9 0.3 fusion.10
  168.3 0.6 fusion.12
  168.8 0.3 fusion.8
  169.2 0.4 convolution_subtract_fusion
  169.6 0.3 fusion.6
  169.9 0.2 fusion.4
  170.2 0.3 convolution_bitcast_fusion
  170.6 8.2 %collective-permute-start.10 = (f32[1,32,512]{2,1,0:T(8,128)S(1)}, f32[1,32,512]{2,1,0:T(8,128)S(1)}, u32[]{:S(2)}, u32[]{:S(2)}) collective-permute-start(f32[1,32,512]{2,1,0:T(8,128)S(1)} %get-tuple-element.33), channel_id=1, source_target_pairs={{0,352},{1,161},{2,354},{3,163},{4,356},{5,165},{6,358},{7,167},{8... | collective-permute-start | bytes 196616 | tf_op jit(solution)/shard_map/ppermute | solution.py:63
  178.8 3.6 %collective-permute-start.14 = (f32[1,32,512]{2,1,0:T(8,128)S(1)}, f32[1,32,512]{2,1,0:T(8,128)S(1)}, u32[]{:S(2)}, u32[]{:S(2)}) collective-permute-start(f32[1,32,512]{2,1,0:T(8,128)S(1)} %get-tuple-element.32), channel_id=1, source_target_pairs={{0,352},{1,161},{2,354},{3,163},{4,356},{5,165},{6,358},{7,167},{8... | collective-permute-start | bytes 196616 | tf_op jit(solution)/shard_map/ppermute | solution.py:63
  182.4 1.4 collective-permute-done.10
  183.8 7.7 %collective-permute-start.11 = (f32[2,32,512]{2,1,0:T(8,128)S(1)}, f32[2,32,512]{2,1,0:T(8,128)S(1)}, u32[]{:S(2)}, u32[]{:S(2)}) collective-permute-start(f32[2,32,512]{2,1,0:T(8,128)S(1)} %pad_maximum_fusion.6), channel_id=1, source_target_pairs={{0,96},{1,417},{2,98},{3,419},{4,100},{5,421},{6,102},{7,423},{8,1... | collective-permute-start | bytes 393224 | tf_op jit(solution)/shard_map/ppermute | solution.py:63
  191.5 4.7 %collective-permute-done.14 = f32[1,32,512]{2,1,0:T(8,128)S(1)} collective-permute-done((f32[1,32,512]{2,1,0:T(8,128)S(1)}, f32[1,32,512]{2,1,0:T(8,128)S(1)}, u32[]{:S(2)}, u32[]{:S(2)}) %collective-permute-start.14) | collective-permute-done | bytes 65568 | tf_op jit(solution)/shard_map/ppermute | solution.py:63
  196.2 1.9 collective-permute-start.15
  198.2 1.9 collective-permute-start.12
  200.1 4.9 %collective-permute-done.15 = f32[2,32,512]{2,1,0:T(8,128)S(1)} collective-permute-done((f32[2,32,512]{2,1,0:T(8,128)S(1)}, f32[2,32,512]{2,1,0:T(8,128)S(1)}, u32[]{:S(2)}, u32[]{:S(2)}) %collective-permute-start.15) | collective-permute-done | bytes 131104 | tf_op jit(solution)/shard_map/ppermute | solution.py:63
  205.0 1.9 collective-permute-start.16
  206.9 3.5 %collective-permute-done.12 = f32[4,32,512]{2,1,0:T(8,128)S(1)} collective-permute-done((f32[4,32,512]{2,1,0:T(8,128)S(1)}, f32[4,32,512]{2,1,0:T(8,128)S(1)}, u32[]{:S(2)}, u32[]{:S(2)}) %collective-permute-start.12) | collective-permute-done | bytes 262176 | tf_op jit(solution)/shard_map/ppermute | solution.py:63
  210.5 1.9 collective-permute-start.13
  212.4 4.8 %collective-permute-done.16 = f32[4,32,512]{2,1,0:T(8,128)S(1)} collective-permute-done((f32[4,32,512]{2,1,0:T(8,128)S(1)}, f32[4,32,512]{2,1,0:T(8,128)S(1)}, u32[]{:S(2)}, u32[]{:S(2)}) %collective-permute-start.16) | collective-permute-done | bytes 262176 | tf_op jit(solution)/shard_map/ppermute | solution.py:63
  217.3 1.9 collective-permute-start.17
  219.2 2.3 collective-permute-done.13.come_ref
  221.6 0.8 copy-done.5
  222.4 9.2 %updated.2.c_ref = f32[1024,512]{1,0:T(8,128)} custom-call(s32[16]{0:T(128)} %and_select_fusion.order_ref, f32[1024,512]{1,0:T(8,128)} %c_ref.3, f32[1024,512]{1,0:T(8,128)} %bitcast.35, f32[8,32,512]{2,1,0:T(8,128)} %copy-done.5, f32[8,32,512]{2,1,0:T(8,128)} %copy-done.1), custom_call_target="tpu_custom_call" | custom-call | flops 1610612736 | bytes 7340032 | tf_op jit(solution)/shard_map/updated/pallas_call | solution.py:158
  231.6 0.8 copy-done.6
  232.4 9.2 %updated.3 = f32[1024,512]{1,0:T(8,128)} custom-call(s32[16]{0:T(128)} %and_select_fusion.order_ref, f32[1024,512]{1,0:T(8,128)} %updated.2.c_ref, f32[1024,512]{1,0:T(8,128)} %collective-permute-done.4.v_ref, f32[8,32,512]{2,1,0:T(8,128)} %copy-done.6, f32[8,32,512]{2,1,0:T(8,128)} %copy-done.2), custom_call_target="tpu_custom_call" | custom-call | flops 1610612736 | bytes 7340032 | tf_op jit(solution)/shard_map/updated/pallas_call | solution.py:158
  (40 shorter events, 0.4 us)
Async XLA Ops:
  35.8 14.1 %copy-start = (f32[32,32,512]{2,1,0:T(8,128)}, f32[32,32,512]{2,1,0:T(8,128)S(1)}, u32[]{:S(2)}) copy-start(f32[32,32,512]{2,1,0:T(8,128)S(1)} %all_to_all.20) | copy-start | bytes 6291460
  35.8 7.2 %collective-permute-start.4 = (f32[1024,512]{1,0:T(8,128)S(1)}, f32[1024,512]{1,0:T(8,128)}, u32[]{:S(2)}, u32[]{:S(2)}) collective-permute-start(f32[1024,512]{1,0:T(8,128)S(1)} %bitcast.31), channel_id=1, source_target_pairs={{0,1},{1,0},{2,3},{3,2},{4,5},{5,4},{6,7},{7,6},{8,9},{9,8},{10,11... | collective-permute-start | bytes 6291464 | tf_op jit(solution)/shard_map/ppermute | solution.py:176
  49.8 43.8 %copy-start.7 = (f32[8,1024]{1,0:T(8,128)S(1)}, f32[8,1024]{1,0:T(8,128)}, u32[]{:S(2)}) copy-start(f32[8,1024]{1,0:T(8,128)} %param.6) | copy-start | bytes 98308
  94.8 32.6 %all-to-all-start.3 = ((f32[32,8,1280]{2,1,0:T(8,128)}), f32[32,8,1280]{2,1,0:T(8,128)S(1)}, u32[]{:S(2)}, u32[]{:S(2)}) async-start(f32[32,8,1280]{2,1,0:T(8,128)} %bitcast.11), calls=%async_computation.3 | async-start | bytes 2621440 | tf_op jit(solution)/shard_map/all_to_all | solution.py:175
  100.1 4.2 %copy-start.8 = (s32[16]{0:T(128)S(1)}, s32[16]{0:T(128)}, u32[]{:S(2)}) copy-start(s32[16]{0:T(128)} %constant.59.clone) | copy-start | bytes 196
  110.7 12.1 %copy-start.4 = (f32[8,32,512]{2,1,0:T(8,128)S(1)}, f32[8,32,512]{2,1,0:T(8,128)}, u32[]{:S(2)}) copy-start(f32[8,32,512]{2,1,0:T(8,128)} %get-tuple-element.13) | copy-start | bytes 1572868
  110.7 12.1 %collective-permute-start = (f32[8,32,512]{2,1,0:T(8,128)}, f32[8,32,512]{2,1,0:T(8,128)}, u32[]{:S(2)}, u32[]{:S(2)}) collective-permute-start(f32[8,32,512]{2,1,0:T(8,128)} %get-tuple-element.14), channel_id=1, source_target_pairs={{0,32},{1,481},{2,34},{3,483},{4,36},{5,485},{6,38},{7,487},{8,40}... | collective-permute-start | bytes 1572872 | tf_op jit(solution)/shard_map/ppermute | solution.py:53
  119.5 13.2 %copy-start.3 = (f32[8,32,512]{2,1,0:T(8,128)S(1)}, f32[8,32,512]{2,1,0:T(8,128)}, u32[]{:S(2)}) copy-start(f32[8,32,512]{2,1,0:T(8,128)} %get-tuple-element.15) | copy-start | bytes 1572868
  119.5 13.2 %collective-permute-start.5 = (f32[8,32,512]{2,1,0:T(8,128)}, f32[8,32,512]{2,1,0:T(8,128)S(1)}, u32[]{:S(2)}, u32[]{:S(2)}) collective-permute-start(f32[8,32,512]{2,1,0:T(8,128)} %get-tuple-element.16), channel_id=1, source_target_pairs={{0,32},{1,481},{2,34},{3,483},{4,36},{5,485},{6,38},{7,487},{8,40}... | collective-permute-start | bytes 1572872 | tf_op jit(solution)/shard_map/ppermute | solution.py:53
  123.9 12.1 %collective-permute-start.1 = (f32[4,32,512]{2,1,0:T(8,128)S(1)}, f32[4,32,512]{2,1,0:T(8,128)S(1)}, u32[]{:S(2)}, u32[]{:S(2)}) collective-permute-start(f32[4,32,512]{2,1,0:T(8,128)S(1)} %get-tuple-element.25), channel_id=1, source_target_pairs={{0,480},{1,33},{2,482},{3,35},{4,484},{5,37},{6,486},{7,39},{8,488... | collective-permute-start | bytes 786440 | tf_op jit(solution)/shard_map/ppermute | solution.py:53
  127.4 40.4 %collective-permute-start.9 = (f32[256,1280]{1,0:T(8,128)S(1)}, f32[256,1280]{1,0:T(8,128)S(1)}, u32[]{:S(2)}, u32[]{:S(2)}) collective-permute-start(f32[256,1280]{1,0:T(8,128)S(1)} %bitcast.37), channel_id=1, source_target_pairs={{0,1},{1,0},{2,3},{3,2},{4,5},{5,4},{6,7},{7,6},{8,9},{9,8},{10,11... | collective-permute-start | bytes 3932168 | tf_op jit(solution)/shard_map/ppermute | solution.py:176
  132.8 12.4 %collective-permute-start.6 = (f32[4,32,512]{2,1,0:T(8,128)S(1)}, f32[4,32,512]{2,1,0:T(8,128)S(1)}, u32[]{:S(2)}, u32[]{:S(2)}) collective-permute-start(f32[4,32,512]{2,1,0:T(8,128)S(1)} %get-tuple-element.23), channel_id=1, source_target_pairs={{0,480},{1,33},{2,482},{3,35},{4,484},{5,37},{6,486},{7,39},{8,488... | collective-permute-start | bytes 786440 | tf_op jit(solution)/shard_map/ppermute | solution.py:53
  136.0 15.8 %collective-permute-start.2 = (f32[2,32,512]{2,1,0:T(8,128)S(1)}, f32[2,32,512]{2,1,0:T(8,128)S(1)}, u32[]{:S(2)}, u32[]{:S(2)}) collective-permute-start(f32[2,32,512]{2,1,0:T(8,128)S(1)} %get-tuple-element.31), channel_id=1, source_target_pairs={{0,96},{1,417},{2,98},{3,419},{4,100},{5,421},{6,102},{7,423},{8,1... | collective-permute-start | bytes 393224 | tf_op jit(solution)/shard_map/ppermute | solution.py:53
  145.2 10.3 %collective-permute-start.7 = (f32[2,32,512]{2,1,0:T(8,128)S(1)}, f32[2,32,512]{2,1,0:T(8,128)S(1)}, u32[]{:S(2)}, u32[]{:S(2)}) collective-permute-start(f32[2,32,512]{2,1,0:T(8,128)S(1)} %get-tuple-element.29), channel_id=1, source_target_pairs={{0,96},{1,417},{2,98},{3,419},{4,100},{5,421},{6,102},{7,423},{8,1... | collective-permute-start | bytes 393224 | tf_op jit(solution)/shard_map/ppermute | solution.py:53
  151.8 12.8 %collective-permute-start.3 = (f32[1,32,512]{2,1,0:T(8,128)S(1)}, f32[1,32,512]{2,1,0:T(8,128)S(1)}, u32[]{:S(2)}, u32[]{:S(2)}) collective-permute-start(f32[1,32,512]{2,1,0:T(8,128)S(1)} %slice_add_fusion.10), channel_id=1, source_target_pairs={{0,352},{1,161},{2,354},{3,163},{4,356},{5,165},{6,358},{7,167},{8... | collective-permute-start | bytes 196616 | tf_op jit(solution)/shard_map/ppermute | solution.py:53
  155.5 12.2 %collective-permute-start.8 = (f32[1,32,512]{2,1,0:T(8,128)S(1)}, f32[1,32,512]{2,1,0:T(8,128)S(1)}, u32[]{:S(2)}, u32[]{:S(2)}) collective-permute-start(f32[1,32,512]{2,1,0:T(8,128)S(1)} %slice_add_fusion.8), channel_id=1, source_target_pairs={{0,352},{1,161},{2,354},{3,163},{4,356},{5,165},{6,358},{7,167},{8... | collective-permute-start | bytes 196616 | tf_op jit(solution)/shard_map/ppermute | solution.py:53
  170.6 13.3 %collective-permute-start.10 = (f32[1,32,512]{2,1,0:T(8,128)S(1)}, f32[1,32,512]{2,1,0:T(8,128)S(1)}, u32[]{:S(2)}, u32[]{:S(2)}) collective-permute-start(f32[1,32,512]{2,1,0:T(8,128)S(1)} %get-tuple-element.33), channel_id=1, source_target_pairs={{0,352},{1,161},{2,354},{3,163},{4,356},{5,165},{6,358},{7,167},{8... | collective-permute-start | bytes 196616 | tf_op jit(solution)/shard_map/ppermute | solution.py:63
  178.8 17.4 %collective-permute-start.14 = (f32[1,32,512]{2,1,0:T(8,128)S(1)}, f32[1,32,512]{2,1,0:T(8,128)S(1)}, u32[]{:S(2)}, u32[]{:S(2)}) collective-permute-start(f32[1,32,512]{2,1,0:T(8,128)S(1)} %get-tuple-element.32), channel_id=1, source_target_pairs={{0,352},{1,161},{2,354},{3,163},{4,356},{5,165},{6,358},{7,167},{8... | collective-permute-start | bytes 196616 | tf_op jit(solution)/shard_map/ppermute | solution.py:63
  183.8 14.3 %collective-permute-start.11 = (f32[2,32,512]{2,1,0:T(8,128)S(1)}, f32[2,32,512]{2,1,0:T(8,128)S(1)}, u32[]{:S(2)}, u32[]{:S(2)}) collective-permute-start(f32[2,32,512]{2,1,0:T(8,128)S(1)} %pad_maximum_fusion.6), channel_id=1, source_target_pairs={{0,96},{1,417},{2,98},{3,419},{4,100},{5,421},{6,102},{7,423},{8,1... | collective-permute-start | bytes 393224 | tf_op jit(solution)/shard_map/ppermute | solution.py:63
  196.2 8.8 %collective-permute-start.15 = (f32[2,32,512]{2,1,0:T(8,128)S(1)}, f32[2,32,512]{2,1,0:T(8,128)S(1)}, u32[]{:S(2)}, u32[]{:S(2)}) collective-permute-start(f32[2,32,512]{2,1,0:T(8,128)S(1)} %pad_maximum_fusion.7), channel_id=1, source_target_pairs={{0,96},{1,417},{2,98},{3,419},{4,100},{5,421},{6,102},{7,423},{8,1... | collective-permute-start | bytes 393224 | tf_op jit(solution)/shard_map/ppermute | solution.py:63
  198.2 12.3 %collective-permute-start.12 = (f32[4,32,512]{2,1,0:T(8,128)S(1)}, f32[4,32,512]{2,1,0:T(8,128)S(1)}, u32[]{:S(2)}, u32[]{:S(2)}) collective-permute-start(f32[4,32,512]{2,1,0:T(8,128)S(1)} %pad_maximum_fusion.4), channel_id=1, source_target_pairs={{0,480},{1,33},{2,482},{3,35},{4,484},{5,37},{6,486},{7,39},{8,488... | collective-permute-start | bytes 786440 | tf_op jit(solution)/shard_map/ppermute | solution.py:63
  205.0 12.3 %collective-permute-start.16 = (f32[4,32,512]{2,1,0:T(8,128)S(1)}, f32[4,32,512]{2,1,0:T(8,128)S(1)}, u32[]{:S(2)}, u32[]{:S(2)}) collective-permute-start(f32[4,32,512]{2,1,0:T(8,128)S(1)} %pad_maximum_fusion.5), channel_id=1, source_target_pairs={{0,480},{1,33},{2,482},{3,35},{4,484},{5,37},{6,486},{7,39},{8,488... | collective-permute-start | bytes 786440 | tf_op jit(solution)/shard_map/ppermute | solution.py:63
  210.5 11.1 %copy-start.1 = (f32[8,32,512]{2,1,0:T(8,128)}, f32[8,32,512]{2,1,0:T(8,128)S(1)}, u32[]{:S(2)}) copy-start(f32[8,32,512]{2,1,0:T(8,128)S(1)} %pad_maximum_fusion.2.held_ref) | copy-start | bytes 1572868
  210.5 11.1 %collective-permute-start.13 = (f32[8,32,512]{2,1,0:T(8,128)S(1)}, f32[8,32,512]{2,1,0:T(8,128)S(1)}, u32[]{:S(2)}, u32[]{:S(2)}) collective-permute-start(f32[8,32,512]{2,1,0:T(8,128)S(1)} %pad_maximum_fusion.2.held_ref), channel_id=1, source_target_pairs={{0,32},{1,481},{2,34},{3,483},{4,36},{5,485},{6,38},{7,487},{8,40}... | collective-permute-start | bytes 1572872 | tf_op jit(solution)/shard_map/ppermute | solution.py:63
  217.3 14.3 %copy-start.2 = (f32[8,32,512]{2,1,0:T(8,128)}, f32[8,32,512]{2,1,0:T(8,128)S(1)}, u32[]{:S(2)}) copy-start(f32[8,32,512]{2,1,0:T(8,128)S(1)} %pad_maximum_fusion.3.held_ref) | copy-start | bytes 1572868
  217.3 14.3 %collective-permute-start.17 = (f32[8,32,512]{2,1,0:T(8,128)S(1)}, f32[8,32,512]{2,1,0:T(8,128)S(1)}, u32[]{:S(2)}, u32[]{:S(2)}) collective-permute-start(f32[8,32,512]{2,1,0:T(8,128)S(1)} %pad_maximum_fusion.3.held_ref), channel_id=1, source_target_pairs={{0,32},{1,481},{2,34},{3,483},{4,36},{5,485},{6,38},{7,487},{8,40}... | collective-permute-start | bytes 1572872 | tf_op jit(solution)/shard_map/ppermute | solution.py:63
  221.6 0.8 copy-start.5
  231.5 0.8 copy-start.6

commit v3 on v2

--- a/solution.py
+++ b/solution.py
@@ -1,5 +1,3 @@
-import functools
-
 import jax
 import jax.numpy as jnp
 from jax import lax
@@ -56,6 +54,11 @@
                 return (kept + come)[0]
             sent = kept[:half] + come[:half]
             kept = kept[half:] + come[half:]
+
+    def summed(self, array):
+        for pairs in self.pairs:
+            array = array + lax.ppermute(array, ("row", "col"), pairs)
+        return array
 
     def gathered(self, array):
         held = array[None]
@@ -98,15 +101,8 @@
     )(c)
 
 
-def projection_kernel(step, order_ref, high_ref, low_ref, v_ref, sent_ref, kept_ref, w_ref, vhigh_ref, vlow_ref):
-    vhigh_ref[...], vlow_ref[...] = parts_of(v_ref[...])
-    v = vhigh_ref[...], vlow_ref[...]
-
-    @pl.loop(0, w_ref.shape[0] // step)
-    def _(i):
-        at = pl.ds(pl.multiple_of(i * step, step), step)
-        w_ref[at, :] = product((high_ref[at, :], low_ref[at, :]), v, (((1,), (0,)), ((), ())))
-
+def projection_kernel(order_ref, high_ref, low_ref, v_ref, sent_ref, kept_ref, w_ref):
+    w_ref[...] = product((high_ref[...], low_ref[...]), parts_of(v_ref[...]), (((1,), (0,)), ((), ())))
     half, size, _ = sent_ref.shape
     for i in range(2 * half):
         at = pl.ds(pl.multiple_of(order_ref[i] * size, size), size)
@@ -119,18 +115,20 @@
 def projection(order, c_parts, v):
     width, height = c_parts[0].shape
     ranks, rest = order.shape[0], v.shape[1]
+    step = min(rest, 256)
     out = jax.ShapeDtypeStruct((ranks // 2, width // ranks, rest), jnp.float32)
-    whole = pl.BlockSpec(memory_space=pltpu.VMEM)
+    out_spec = pl.BlockSpec((ranks // 2, width // ranks, step), lambda i, order: (0, 0, i))
+    c_spec = pl.BlockSpec((width, height), lambda i, order: (0, 0))
     return pl.pallas_call(
-        functools.partial(projection_kernel, min(width, 128)),
-        in_specs=[pl.BlockSpec(memory_space=pltpu.SMEM), whole, whole, whole],
-        out_specs=[whole, whole],
+        projection_kernel,
+        grid_spec=pltpu.PrefetchScalarGridSpec(
+            num_scalar_prefetch=1,
+            grid=(rest // step,),
+            in_specs=[c_spec, c_spec, pl.BlockSpec((height, step), lambda i, order: (0, i))],
+            out_specs=[out_spec, out_spec],
+            scratch_shapes=[pltpu.VMEM((width, step), jnp.float32)],
+        ),
         out_shape=[out, out],
-        scratch_shapes=[
-            pltpu.VMEM((width, rest), jnp.float32),
-            pltpu.VMEM((height, rest), jnp.bfloat16),
-            pltpu.VMEM((height, rest), jnp.bfloat16),
-        ],
         cost_estimate=pl.CostEstimate(
             flops=6 * width * height * rest, bytes_accessed=4 * (2 * width * rest + height * (width + rest)), transcendentals=0
         ),
@@ -138,29 +136,35 @@
     )(order, *c_parts, v)
 
 
-def update_kernel(step, order_ref, c_ref, v_ref, come_ref, held_ref, out_ref, high_ref, low_ref):
-    half, size, _ = come_ref.shape
-    for i in range(2 * half):
-        at = pl.ds(pl.multiple_of(order_ref[i] * size, size), size)
-        high_ref[at, :], low_ref[at, :] = parts_of(come_ref[i] if i < half else held_ref[i - half])
-    y = high_ref[...], low_ref[...]
-
-    @pl.loop(0, c_ref.shape[0] // step)
-    def _(i):
-        at = pl.ds(pl.multiple_of(i * step, step), step)
-        out_ref[at, :] = c_ref[at, :] - product(parts_of(v_ref[at, :]), y, (((1,), (1,)), ((), ())))
+def update_kernel(order_ref, c_ref, v_ref, come_ref, held_ref, out_ref, placed_ref, high_ref, low_ref):
+    @pl.when(pl.program_id(0) == 0)
+    def _():
+        half, size, _ = come_ref.shape
+        for i in range(2 * half):
+            at = pl.ds(pl.multiple_of(order_ref[i] * size, size), size)
+            placed_ref[at, :] = come_ref[i] if i < half else held_ref[i - half]
+        high_ref[...], low_ref[...] = parts_of(placed_ref[...].T)
+
+    v, y = parts_of(v_ref[...]), (high_ref[...], low_ref[...])
+    out_ref[...] = c_ref[...] - product(v, y, (((1,), (0,)), ((), ())))
 
 
 def updated(order, c, v, come, held):
     height, width = c.shape
     rest = v.shape[1]
-    whole = pl.BlockSpec(memory_space=pltpu.VMEM)
+    step = min(height, 512)
+    y_spec = pl.BlockSpec(come.shape, lambda i, order: (0, 0, 0))
+    c_spec = pl.BlockSpec((step, width), lambda i, order: (i, 0))
     return pl.pallas_call(
-        functools.partial(update_kernel, min(height, 128)),
-        in_specs=[pl.BlockSpec(memory_space=pltpu.SMEM), whole, whole, whole, whole],
-        out_specs=whole,
+        update_kernel,
+        grid_spec=pltpu.PrefetchScalarGridSpec(
+            num_scalar_prefetch=1,
+            grid=(height // step,),
+            in_specs=[c_spec, pl.BlockSpec((step, rest), lambda i, order: (i, 0)), y_spec, y_spec],
+            out_specs=c_spec,
+            scratch_shapes=[pltpu.VMEM((width, rest), jnp.float32)] + [pltpu.VMEM((rest, width), jnp.bfloat16)] * 2,
+        ),
         out_shape=jax.ShapeDtypeStruct((height, width), jnp.float32),
-        scratch_shapes=[pltpu.VMEM((width, rest), jnp.bfloat16)] * 2,
         cost_estimate=pl.CostEstimate(
             flops=6 * width * height * rest, bytes_accessed=4 * (width * rest + height * (2 * width + rest)), transcendentals=0
         ),
@@ -174,17 +178,6 @@
     sent = jnp.broadcast_to(halves[None], (cols // 2, 2, height, width // 2)).reshape(cols, height, width // 2)
     own = lax.all_to_all(sent, "col", 0, 0, tiled=True).reshape(cols * height, width // 2)
     return own, lax.ppermute(own, "col", [(i, i ^ 1) for i in range(cols)])
-
-
-def summed_over_rows(array, rows):
-    height, width = array.shape
-    tiles = -(-width // (128 * rows)) * rows
-    padded = jnp.pad(array, ((0, 0), (0, tiles * 128 - width)))
-    parts = jnp.moveaxis(padded.reshape(height, rows, -1), 1, 0)
-    part = lax.all_to_all(parts, "row", 0, 0, tiled=True)
-    sent = jnp.broadcast_to(part.sum(axis=0)[None], parts.shape)
-    whole = lax.all_to_all(sent, "row", 0, 0, tiled=True)
-    return jnp.moveaxis(whole, 0, 1).reshape(height, -1)[:, :width]
 
 
 def per_device(weight_basis, panels, factors):
@@ -225,7 +218,7 @@
         axis=1,
     )
     gram = [gram[(j - 1) * slab : j * slab, : j * block] for j in range(1, blocks)]
-    gram = summed_over_rows(jnp.concatenate(gram, axis=1), rows)
+    gram = over_rows.summed(jnp.concatenate(gram, axis=1))
     small = jnp.concatenate(natural(*gathered_halves(jnp.concatenate([gram, factors], axis=1), cols)), axis=1)
 
     left = jnp.concatenate(natural(w_own, w_other), axis=1)

time: 243 us -> 229 us (0.942)
  blocking collectives: 77 us -> 34.4 us
  starting transfers between devices: 73.4 us -> 104 us
  Pallas kernels: 34.4 us -> 26.8 us
  waiting for transfers between devices: 39.4 us -> 45.7 us
    all_to_all x2 -> x0, blocking collectives: 42.5 us -> none  [the longest x1 27.1 us: summed_over_rows(): part = lax.all_to_all(parts, 'row', 0, 0, tiled=True)]
    ppermute x0 -> x4, starting transfers between devices: none -> 22.7 us  [summed(): array = array + lax.ppermute(array, ('row', 'col'), pairs)]
    ppermute x0 -> x4, waiting for transfers between devices: none -> 15.3 us  [summed(): array = array + lax.ppermute(array, ('row', 'col'), pairs)]
    ppermute x8, waiting for transfers between devices: 21.6 us -> 12.8 us  [gathered(): come = lax.ppermute(held, ('row', 'col'), pairs)]
    pallas_call x4, Pallas kernels: 30.3 us -> 22.6 us  [the longest x2 11.8 us: updated(): pl.pallas_call(update_kernel, grid_spec=pltpu.PrefetchScalarGridSpec(num_...]
    ppermute x8, starting transfers between devices: 29.1 us -> 35.2 us  [gathered(): come = lax.ppermute(held, ('row', 'col'), pairs)]
  transfers between devices with their start and end apart: 19 -> 23, of which waited for: 12 -> 15; matrix products, arithmetic and copies ran while one was open for 1% -> 1% of each run, Pallas kernels for 10% -> 9%
where the time goes in v3:
time: 229 us; the launch traced here: 228 us
  starting transfers between devices  104 us (45%)
  waiting for transfers between devices  45.7 us (20%)
  blocking collectives  34.4 us (15%)
  Pallas kernels  26.8 us (12%)
  matrix products  6.41 us (3%)
  local copies, waits for them, and re-layouts  5.68 us (2%)
  other arithmetic  4.84 us (2%)
    ppermute x8, starting transfers between devices, gathered(): come = lax.ppermute(held, ('row', 'col'), pairs)  35.2 us
    ppermute x8, starting transfers between devices, scattered(): come = lax.ppermute(sent, ('row', 'col'), pairs)  35 us
    all_to_all x1, blocking collectives, gathered_halves(): lax.all_to_all(sent, 'col', 0, 0, tiled=True)  34.4 us
    ppermute x4, starting transfers between devices, summed(): array = array + lax.ppermute(array, ('row', 'col'), pairs)  22.7 us
    ppermute x4, waiting for transfers between devices, summed(): array = array + lax.ppermute(array, ('row', 'col'), pairs)  15.3 us
    ppermute x8, waiting for transfers between devices, scattered(): come = lax.ppermute(sent, ('row', 'col'), pairs)  13.7 us
    ppermute x8, waiting for transfers between devices, gathered(): come = lax.ppermute(held, ('row', 'col'), pairs)  12.8 us
    pallas_call x2, Pallas kernels, updated(): pl.pallas_call(update_kernel, grid_spec=pltpu.PrefetchScalarGridSpec(num_...  11.8 us
  transfers between devices with their start and end apart: 23, of which 15 were waited for; matrix products, arithmetic and copies ran while one was open for 1% of the time, Pallas kernels for 9%

profile of v3, /device:TPU:6, one launch (start us, length us, event | category | flops | bytes accessed | tf_op | source)
XLA Modules:
  0.0 228.0 jit_solution(14879804695469201352)
XLA Ops:
  0.0 1.0 reshape.134
  1.1 0.2 broadcast_in_dim.4
  1.3 34.4 %all_to_all.10 = f32[32,32,512]{2,1,0:T(8,128)S(1)} all-to-all(f32[32,32,512]{2,1,0:T(8,128)S(1)} %bitcast.29), channel_id=1, replica_groups=mesh['row'=16,'col'=32] {'col'}, dimensions={0} | all-to-all | bytes 4194304 | tf_op jit(solution)/shard_map/all_to_all | solution.py:179
  35.8 3.3 %collective-permute-start.4 = (f32[1024,512]{1,0:T(8,128)S(1)}, f32[1024,512]{1,0:T(8,128)}, u32[]{:S(2)}, u32[]{:S(2)}) collective-permute-start(f32[1024,512]{1,0:T(8,128)S(1)} %bitcast.24), channel_id=1, source_target_pairs={{0,1},{1,0},{2,3},{3,2},{4,5},{5,4},{6,7},{7,6},{8,9},{9,8},{10,11... | collective-permute-start | bytes 6291464 | tf_op jit(solution)/shard_map/ppermute | solution.py:180
  39.1 3.9 %collective-permute-done.4.v_ref = f32[1024,512]{1,0:T(8,128)} collective-permute-done((f32[1024,512]{1,0:T(8,128)S(1)}, f32[1024,512]{1,0:T(8,128)}, u32[]{:S(2)}, u32[]{:S(2)}) %collective-permute-start.4) | collective-permute-done | bytes 2097184 | tf_op jit(solution)/shard_map/ppermute | solution.py:180
  42.9 2.6 %dynamic-slice_select_fusion.2 = (f32[1024,8]{1,0:T(8,128)}, f32[1024,8]{1,0:T(8,128)S(1)}, f32[1024,8]{1,0:T(8,128)S(1)}) fusion(f32[1024,512]{1,0:T(8,128)} %collective-permute-done.4.v_ref, s32[]{:T(128)S(6)} %select_n.125, f32[1024,512]{1,0:T(8,128)S(1)} %bitcast.25, pred[]{:T(512)S(6)} %eq.16, pred[]{:T(512)S(6)} %eq.17, s32[]{:T(128)S(6)} %select_n.128), kind=kLoop, calls=%fused_computation.12 | loop fusion | flops 24576 | bytes 229386 | tf_op jit(solution)/shard_map/jit(_where)/select_n | solution.py:210
  45.6 1.2 copy.7
  46.9 0.2 copy.8
  47.1 2.7 %fusion.13 = f32[24,512]{1,0:T(8,128)S(1)} fusion(f32[1024,512]{1,0:T(8,128)} %collective-permute-done.4.v_ref, f32[1024,8]{0,1:T(8,128)S(1)} %copy.9, f32[1024,8]{0,1:T(8,128)S(1)} %copy.8, f32[1024,8]{0,1:T(8,128)S(1)} %copy.7), kind=kOutput, calls=%fused_computation.38 | convolution fusion | flops 151044096 | bytes 2244608 | tf_op jit(solution)/shard_map/dot_general | solution.py:216
  49.8 1.1 broadcast_select_fusion.3
  51.0 2.6 %collective-permute-start.9 = (f32[8,1536]{1,0:T(8,128)S(1)}, f32[8,1536]{1,0:T(8,128)S(1)}, u32[]{:S(2)}, u32[]{:S(2)}) collective-permute-start(f32[8,1536]{1,0:T(8,128)S(1)} %fusion.19), channel_id=1, source_target_pairs={{0,32},{1,481},{2,34},{3,483},{4,36},{5,485},{6,38},{7,487},{8,40}... | collective-permute-start | bytes 147464 | tf_op jit(solution)/shard_map/ppermute | solution.py:60
  53.6 3.4 %collective-permute-done.9 = f32[8,1536]{1,0:T(8,128)S(1)} collective-permute-done((f32[8,1536]{1,0:T(8,128)S(1)}, f32[8,1536]{1,0:T(8,128)S(1)}, u32[]{:S(2)}, u32[]{:S(2)}) %collective-permute-start.9) | collective-permute-done | bytes 49184 | tf_op jit(solution)/shard_map/ppermute | solution.py:60
  57.0 10.2 %collective-permute-start.10 = (f32[8,1536]{1,0:T(8,128)S(1)}, f32[8,1536]{1,0:T(8,128)S(1)}, u32[]{:S(2)}, u32[]{:S(2)}) collective-permute-start(f32[8,1536]{1,0:T(8,128)S(1)} %add.115), channel_id=1, source_target_pairs={{0,480},{1,33},{2,482},{3,35},{4,484},{5,37},{6,486},{7,39},{8,488... | collective-permute-start | bytes 147464 | tf_op jit(solution)/shard_map/ppermute | solution.py:60
  67.2 2.1 collective-permute-done.10
  69.2 1.9 collective-permute-start.11
  71.1 5.9 %collective-permute-done.11 = f32[8,1536]{1,0:T(8,128)S(1)} collective-permute-done((f32[8,1536]{1,0:T(8,128)S(1)}, f32[8,1536]{1,0:T(8,128)S(1)}, u32[]{:S(2)}, u32[]{:S(2)}) %collective-permute-start.11) | collective-permute-done | bytes 49184 | tf_op jit(solution)/shard_map/ppermute | solution.py:60
  77.0 8.1 %collective-permute-start.12 = (f32[8,1536]{1,0:T(8,128)S(1)}, f32[8,1536]{1,0:T(8,128)S(1)}, u32[]{:S(2)}, u32[]{:S(2)}) collective-permute-start(f32[8,1536]{1,0:T(8,128)S(1)} %add.117), channel_id=1, source_target_pairs={{0,352},{1,161},{2,354},{3,163},{4,356},{5,165},{6,358},{7,167},{8... | collective-permute-start | bytes 147464 | tf_op jit(solution)/shard_map/ppermute | solution.py:60
  85.1 3.9 %collective-permute-done.12 = f32[8,1536]{1,0:T(8,128)S(1)} collective-permute-done((f32[8,1536]{1,0:T(8,128)S(1)}, f32[8,1536]{1,0:T(8,128)S(1)}, u32[]{:S(2)}, u32[]{:S(2)}) %collective-permute-start.12) | collective-permute-done | bytes 49184 | tf_op jit(solution)/shard_map/ppermute | solution.py:60
  89.1 1.2 broadcast_in_dim.5
  90.3 5.5 %all-to-all-start.1 = ((f32[32,8,1280]{2,1,0:T(8,128)}), f32[32,8,1280]{2,1,0:T(8,128)S(1)}, u32[]{:S(2)}, u32[]{:S(2)}) async-start(f32[32,8,1280]{2,1,0:T(8,128)} %bitcast.7), calls=%async_computation.1 | async-start | bytes 2621440 | tf_op jit(solution)/shard_map/all_to_all | solution.py:179
  95.8 4.1 %turned.1 = (bf16[512,1024]{1,0:T(8,128)(2,1)}, bf16[512,1024]{1,0:T(8,128)(2,1)}) custom-call(f32[1024,512]{1,0:T(8,128)} %c_ref.3), custom_call_target="tpu_custom_call" | custom-call | flops 4194304 | bytes 4194304 | tf_op jit(solution)/shard_map/turned/pallas_call | solution.py:93
  99.9 0.5 and_select_fusion.order_ref
  100.4 5.4 %projection.2 = (f32[8,32,512]{2,1,0:T(8,128)}, f32[8,32,512]{2,1,0:T(8,128)}) custom-call(s32[16]{0:T(128)} %and_select_fusion.order_ref, bf16[512,1024]{1,0:T(8,128)(2,1)} %get-tuple-element.11.high_ref, bf16[512,1024]{1,0:T(8,128)(2,1)} %get-tuple-element.12.low_ref, f32[1024,512]{1,0:T(8,128)} %bitcast.27), custom_call_target="tpu_custom_call" | custom-call | flops 1610612736 | bytes 6291456 | tf_op jit(solution)/shard_map/projection/pallas_call | solution.py:122
  105.9 2.0 collective-permute-start
  107.9 5.4 %projection.3 = (f32[8,32,512]{2,1,0:T(8,128)}, f32[8,32,512]{2,1,0:T(8,128)}) custom-call(s32[16]{0:T(128)} %and_select_fusion.order_ref, bf16[512,1024]{1,0:T(8,128)(2,1)} %get-tuple-element.11.high_ref, bf16[512,1024]{1,0:T(8,128)(2,1)} %get-tuple-element.12.low_ref, f32[1024,512]{1,0:T(8,128)} %collective-permute-done.4.v_ref), custom_call_target="tpu_custom_call" | custom-call | flops 1610612736 | bytes 6291456 | tf_op jit(solution)/shard_map/projection/pallas_call | solution.py:122
  113.4 4.0 %collective-permute-start.5 = (f32[8,32,512]{2,1,0:T(8,128)}, f32[8,32,512]{2,1,0:T(8,128)S(1)}, u32[]{:S(2)}, u32[]{:S(2)}) collective-permute-start(f32[8,32,512]{2,1,0:T(8,128)} %get-tuple-element.16), channel_id=1, source_target_pairs={{0,32},{1,481},{2,34},{3,483},{4,36},{5,485},{6,38},{7,487},{8,40}... | collective-permute-start | bytes 1572872 | tf_op jit(solution)/shard_map/ppermute | solution.py:51
  117.4 1.1 slice_add_fusion.3
  118.5 5.1 %collective-permute-start.1 = (f32[4,32,512]{2,1,0:T(8,128)S(1)}, f32[4,32,512]{2,1,0:T(8,128)S(1)}, u32[]{:S(2)}, u32[]{:S(2)}) collective-permute-start(f32[4,32,512]{2,1,0:T(8,128)S(1)} %get-tuple-element.25), channel_id=1, source_target_pairs={{0,480},{1,33},{2,482},{3,35},{4,484},{5,37},{6,486},{7,39},{8,488... | collective-permute-start | bytes 786440 | tf_op jit(solution)/shard_map/ppermute | solution.py:51
  123.6 1.9 collective-permute-start.13
  125.6 1.3 collective-permute-done.5
  126.9 5.3 %collective-permute-start.6 = (f32[4,32,512]{2,1,0:T(8,128)S(1)}, f32[4,32,512]{2,1,0:T(8,128)S(1)}, u32[]{:S(2)}, u32[]{:S(2)}) collective-permute-start(f32[4,32,512]{2,1,0:T(8,128)S(1)} %get-tuple-element.23), channel_id=1, source_target_pairs={{0,480},{1,33},{2,482},{3,35},{4,484},{5,37},{6,486},{7,39},{8,488... | collective-permute-start | bytes 786440 | tf_op jit(solution)/shard_map/ppermute | solution.py:51
  132.3 1.9 collective-permute-start.2
  134.2 3.0 %collective-permute-done.6 = f32[4,32,512]{2,1,0:T(8,128)S(1)} collective-permute-done((f32[4,32,512]{2,1,0:T(8,128)S(1)}, f32[4,32,512]{2,1,0:T(8,128)S(1)}, u32[]{:S(2)}, u32[]{:S(2)}) %collective-permute-start.6) | collective-permute-done | bytes 262176 | tf_op jit(solution)/shard_map/ppermute | solution.py:51
  137.3 2.7 %collective-permute-start.7 = (f32[2,32,512]{2,1,0:T(8,128)S(1)}, f32[2,32,512]{2,1,0:T(8,128)S(1)}, u32[]{:S(2)}, u32[]{:S(2)}) collective-permute-start(f32[2,32,512]{2,1,0:T(8,128)S(1)} %get-tuple-element.29), channel_id=1, source_target_pairs={{0,96},{1,417},{2,98},{3,419},{4,100},{5,421},{6,102},{7,423},{8,1... | collective-permute-start | bytes 393224 | tf_op jit(solution)/shard_map/ppermute | solution.py:51
  140.0 1.4 collective-permute-done.2
  141.4 9.3 %collective-permute-start.3 = (f32[1,32,512]{2,1,0:T(8,128)S(1)}, f32[1,32,512]{2,1,0:T(8,128)S(1)}, u32[]{:S(2)}, u32[]{:S(2)}) collective-permute-start(f32[1,32,512]{2,1,0:T(8,128)S(1)} %slice_add_fusion.10), channel_id=1, source_target_pairs={{0,352},{1,161},{2,354},{3,163},{4,356},{5,165},{6,358},{7,167},{8... | collective-permute-start | bytes 196616 | tf_op jit(solution)/shard_map/ppermute | solution.py:51
  150.7 4.6 %collective-permute-start.8 = (f32[1,32,512]{2,1,0:T(8,128)S(1)}, f32[1,32,512]{2,1,0:T(8,128)S(1)}, u32[]{:S(2)}, u32[]{:S(2)}) collective-permute-start(f32[1,32,512]{2,1,0:T(8,128)S(1)} %slice_add_fusion.8), channel_id=1, source_target_pairs={{0,352},{1,161},{2,354},{3,163},{4,356},{5,165},{6,358},{7,167},{8... | collective-permute-start | bytes 196616 | tf_op jit(solution)/shard_map/ppermute | solution.py:51
  155.3 8.1 %collective-permute-done.8 = f32[1,32,512]{2,1,0:T(8,128)S(1)} collective-permute-done((f32[1,32,512]{2,1,0:T(8,128)S(1)}, f32[1,32,512]{2,1,0:T(8,128)S(1)}, u32[]{:S(2)}, u32[]{:S(2)}) %collective-permute-start.8) | collective-permute-done | bytes 65568 | tf_op jit(solution)/shard_map/ppermute | solution.py:51
  163.4 0.2 broadcast_select_fusion
  163.6 0.3 fusion.10
  163.9 0.6 fusion.12
  164.5 0.3 fusion.8
  164.9 0.4 convolution_subtract_fusion
  165.3 0.3 fusion.6
  165.6 0.2 fusion.4
  165.9 0.3 convolution_bitcast_fusion
  166.2 4.1 %collective-permute-start.14 = (f32[1,32,512]{2,1,0:T(8,128)S(1)}, f32[1,32,512]{2,1,0:T(8,128)S(1)}, u32[]{:S(2)}, u32[]{:S(2)}) collective-permute-start(f32[1,32,512]{2,1,0:T(8,128)S(1)} %get-tuple-element.33), channel_id=1, source_target_pairs={{0,352},{1,161},{2,354},{3,163},{4,356},{5,165},{6,358},{7,167},{8... | collective-permute-start | bytes 196616 | tf_op jit(solution)/shard_map/ppermute | solution.py:66
  170.3 7.8 %collective-permute-start.18 = (f32[1,32,512]{2,1,0:T(8,128)S(1)}, f32[1,32,512]{2,1,0:T(8,128)S(1)}, u32[]{:S(2)}, u32[]{:S(2)}) collective-permute-start(f32[1,32,512]{2,1,0:T(8,128)S(1)} %get-tuple-element.32), channel_id=1, source_target_pairs={{0,352},{1,161},{2,354},{3,163},{4,356},{5,165},{6,358},{7,167},{8... | collective-permute-start | bytes 196616 | tf_op jit(solution)/shard_map/ppermute | solution.py:66
  178.1 2.2 collective-permute-done.14
  180.3 3.1 %collective-permute-start.15 = (f32[2,32,512]{2,1,0:T(8,128)S(1)}, f32[2,32,512]{2,1,0:T(8,128)S(1)}, u32[]{:S(2)}, u32[]{:S(2)}) collective-permute-start(f32[2,32,512]{2,1,0:T(8,128)S(1)} %pad_maximum_fusion.6), channel_id=1, source_target_pairs={{0,96},{1,417},{2,98},{3,419},{4,100},{5,421},{6,102},{7,423},{8,1... | collective-permute-start | bytes 393224 | tf_op jit(solution)/shard_map/ppermute | solution.py:66
  183.4 1.5 collective-permute-done.18
  184.9 3.7 %collective-permute-start.19 = (f32[2,32,512]{2,1,0:T(8,128)S(1)}, f32[2,32,512]{2,1,0:T(8,128)S(1)}, u32[]{:S(2)}, u32[]{:S(2)}) collective-permute-start(f32[2,32,512]{2,1,0:T(8,128)S(1)} %pad_maximum_fusion.7), channel_id=1, source_target_pairs={{0,96},{1,417},{2,98},{3,419},{4,100},{5,421},{6,102},{7,423},{8,1... | collective-permute-start | bytes 393224 | tf_op jit(solution)/shard_map/ppermute | solution.py:66
  188.7 0.6 collective-permute-done.15
  189.3 2.1 collective-permute-start.16
  191.4 4.9 %collective-permute-done.19 = f32[2,32,512]{2,1,0:T(8,128)S(1)} collective-permute-done((f32[2,32,512]{2,1,0:T(8,128)S(1)}, f32[2,32,512]{2,1,0:T(8,128)S(1)}, u32[]{:S(2)}, u32[]{:S(2)}) %collective-permute-start.19) | collective-permute-done | bytes 131104 | tf_op jit(solution)/shard_map/ppermute | solution.py:66
  196.3 4.0 %collective-permute-start.20 = (f32[4,32,512]{2,1,0:T(8,128)S(1)}, f32[4,32,512]{2,1,0:T(8,128)S(1)}, u32[]{:S(2)}, u32[]{:S(2)}) collective-permute-start(f32[4,32,512]{2,1,0:T(8,128)S(1)} %pad_maximum_fusion.5), channel_id=1, source_target_pairs={{0,480},{1,33},{2,482},{3,35},{4,484},{5,37},{6,486},{7,39},{8,488... | collective-permute-start | bytes 786440 | tf_op jit(solution)/shard_map/ppermute | solution.py:66
  200.4 4.6 %collective-permute-start.17 = (f32[8,32,512]{2,1,0:T(8,128)S(1)}, f32[8,32,512]{2,1,0:T(8,128)S(1)}, u32[]{:S(2)}, u32[]{:S(2)}) collective-permute-start(f32[8,32,512]{2,1,0:T(8,128)S(1)} %pad_maximum_fusion.2.held_ref), channel_id=1, source_target_pairs={{0,32},{1,481},{2,34},{3,483},{4,36},{5,485},{6,38},{7,487},{8,40}... | collective-permute-start | bytes 1572872 | tf_op jit(solution)/shard_map/ppermute | solution.py:66
  205.0 3.3 %collective-permute-done.20 = f32[4,32,512]{2,1,0:T(8,128)S(1)} collective-permute-done((f32[4,32,512]{2,1,0:T(8,128)S(1)}, f32[4,32,512]{2,1,0:T(8,128)S(1)}, u32[]{:S(2)}, u32[]{:S(2)}) %collective-permute-start.20) | collective-permute-done | bytes 262176 | tf_op jit(solution)/shard_map/ppermute | solution.py:66
  208.3 5.8 %collective-permute-start.21 = (f32[8,32,512]{2,1,0:T(8,128)S(1)}, f32[8,32,512]{2,1,0:T(8,128)S(1)}, u32[]{:S(2)}, u32[]{:S(2)}) collective-permute-start(f32[8,32,512]{2,1,0:T(8,128)S(1)} %pad_maximum_fusion.3.held_ref), channel_id=1, source_target_pairs={{0,32},{1,481},{2,34},{3,483},{4,36},{5,485},{6,38},{7,487},{8,40}... | collective-permute-start | bytes 1572872 | tf_op jit(solution)/shard_map/ppermute | solution.py:66
  214.1 0.8 copy-done.5
  214.9 5.9 %updated.2.c_ref = f32[1024,512]{1,0:T(8,128)} custom-call(s32[16]{0:T(128)} %and_select_fusion.order_ref, f32[1024,512]{1,0:T(8,128)} %c_ref.3, f32[1024,512]{1,0:T(8,128)} %bitcast.28, f32[8,32,512]{2,1,0:T(8,128)} %copy-done.5, f32[8,32,512]{2,1,0:T(8,128)} %copy-done.1), custom_call_target="tpu_custom_call" | custom-call | flops 1610612736 | bytes 7340032 | tf_op jit(solution)/shard_map/updated/pallas_call | solution.py:158
  220.8 0.4 collective-permute-done.21.come_ref
  221.2 0.8 copy-done.6
  222.1 5.9 %updated.3 = f32[1024,512]{1,0:T(8,128)} custom-call(s32[16]{0:T(128)} %and_select_fusion.order_ref, f32[1024,512]{1,0:T(8,128)} %updated.2.c_ref, f32[1024,512]{1,0:T(8,128)} %collective-permute-done.4.v_ref, f32[8,32,512]{2,1,0:T(8,128)} %copy-done.6, f32[8,32,512]{2,1,0:T(8,128)} %copy-done.2), custom_call_target="tpu_custom_call" | custom-call | flops 1610612736 | bytes 7340032 | tf_op jit(solution)/shard_map/updated/pallas_call | solution.py:158
  (47 shorter events, 0.7 us)
Async XLA Ops:
  35.8 14.1 %copy-start = (f32[32,32,512]{2,1,0:T(8,128)}, f32[32,32,512]{2,1,0:T(8,128)S(1)}, u32[]{:S(2)}) copy-start(f32[32,32,512]{2,1,0:T(8,128)S(1)} %all_to_all.10) | copy-start | bytes 6291460
  35.8 7.2 %collective-permute-start.4 = (f32[1024,512]{1,0:T(8,128)S(1)}, f32[1024,512]{1,0:T(8,128)}, u32[]{:S(2)}, u32[]{:S(2)}) collective-permute-start(f32[1024,512]{1,0:T(8,128)S(1)} %bitcast.24), channel_id=1, source_target_pairs={{0,1},{1,0},{2,3},{3,2},{4,5},{5,4},{6,7},{7,6},{8,9},{9,8},{10,11... | collective-permute-start | bytes 6291464 | tf_op jit(solution)/shard_map/ppermute | solution.py:180
  49.8 39.2 %copy-start.7 = (f32[8,1024]{1,0:T(8,128)S(1)}, f32[8,1024]{1,0:T(8,128)}, u32[]{:S(2)}) copy-start(f32[8,1024]{1,0:T(8,128)} %param.6) | copy-start | bytes 98308
  51.0 6.0 %collective-permute-start.9 = (f32[8,1536]{1,0:T(8,128)S(1)}, f32[8,1536]{1,0:T(8,128)S(1)}, u32[]{:S(2)}, u32[]{:S(2)}) collective-permute-start(f32[8,1536]{1,0:T(8,128)S(1)} %fusion.19), channel_id=1, source_target_pairs={{0,32},{1,481},{2,34},{3,483},{4,36},{5,485},{6,38},{7,487},{8,40}... | collective-permute-start | bytes 147464 | tf_op jit(solution)/shard_map/ppermute | solution.py:60
  57.0 12.2 %collective-permute-start.10 = (f32[8,1536]{1,0:T(8,128)S(1)}, f32[8,1536]{1,0:T(8,128)S(1)}, u32[]{:S(2)}, u32[]{:S(2)}) collective-permute-start(f32[8,1536]{1,0:T(8,128)S(1)} %add.115), channel_id=1, source_target_pairs={{0,480},{1,33},{2,482},{3,35},{4,484},{5,37},{6,486},{7,39},{8,488... | collective-permute-start | bytes 147464 | tf_op jit(solution)/shard_map/ppermute | solution.py:60
  69.2 7.8 %collective-permute-start.11 = (f32[8,1536]{1,0:T(8,128)S(1)}, f32[8,1536]{1,0:T(8,128)S(1)}, u32[]{:S(2)}, u32[]{:S(2)}) collective-permute-start(f32[8,1536]{1,0:T(8,128)S(1)} %add.116), channel_id=1, source_target_pairs={{0,96},{1,417},{2,98},{3,419},{4,100},{5,421},{6,102},{7,423},{8,1... | collective-permute-start | bytes 147464 | tf_op jit(solution)/shard_map/ppermute | solution.py:60
  77.0 12.0 %collective-permute-start.12 = (f32[8,1536]{1,0:T(8,128)S(1)}, f32[8,1536]{1,0:T(8,128)S(1)}, u32[]{:S(2)}, u32[]{:S(2)}) collective-permute-start(f32[8,1536]{1,0:T(8,128)S(1)} %add.117), channel_id=1, source_target_pairs={{0,352},{1,161},{2,354},{3,163},{4,356},{5,165},{6,358},{7,167},{8... | collective-permute-start | bytes 147464 | tf_op jit(solution)/shard_map/ppermute | solution.py:60
  90.3 33.4 %all-to-all-start.1 = ((f32[32,8,1280]{2,1,0:T(8,128)}), f32[32,8,1280]{2,1,0:T(8,128)S(1)}, u32[]{:S(2)}, u32[]{:S(2)}) async-start(f32[32,8,1280]{2,1,0:T(8,128)} %bitcast.7), calls=%async_computation.1 | async-start | bytes 2621440 | tf_op jit(solution)/shard_map/all_to_all | solution.py:179
  95.7 4.2 %copy-start.8 = (s32[16]{0:T(128)S(1)}, s32[16]{0:T(128)}, u32[]{:S(2)}) copy-start(s32[16]{0:T(128)} %constant.56.clone) | copy-start | bytes 196
  105.9 11.5 %copy-start.4 = (f32[8,32,512]{2,1,0:T(8,128)S(1)}, f32[8,32,512]{2,1,0:T(8,128)}, u32[]{:S(2)}) copy-start(f32[8,32,512]{2,1,0:T(8,128)} %get-tuple-element.13) | copy-start | bytes 1572868
  105.9 11.5 %collective-permute-start = (f32[8,32,512]{2,1,0:T(8,128)}, f32[8,32,512]{2,1,0:T(8,128)}, u32[]{:S(2)}, u32[]{:S(2)}) collective-permute-start(f32[8,32,512]{2,1,0:T(8,128)} %get-tuple-element.14), channel_id=1, source_target_pairs={{0,32},{1,481},{2,34},{3,483},{4,36},{5,485},{6,38},{7,487},{8,40}... | collective-permute-start | bytes 1572872 | tf_op jit(solution)/shard_map/ppermute | solution.py:51
  113.4 13.5 %copy-start.3 = (f32[8,32,512]{2,1,0:T(8,128)S(1)}, f32[8,32,512]{2,1,0:T(8,128)}, u32[]{:S(2)}) copy-start(f32[8,32,512]{2,1,0:T(8,128)} %get-tuple-element.15) | copy-start | bytes 1572868
  113.4 13.5 %collective-permute-start.5 = (f32[8,32,512]{2,1,0:T(8,128)}, f32[8,32,512]{2,1,0:T(8,128)S(1)}, u32[]{:S(2)}, u32[]{:S(2)}) collective-permute-start(f32[8,32,512]{2,1,0:T(8,128)} %get-tuple-element.16), channel_id=1, source_target_pairs={{0,32},{1,481},{2,34},{3,483},{4,36},{5,485},{6,38},{7,487},{8,40}... | collective-permute-start | bytes 1572872 | tf_op jit(solution)/shard_map/ppermute | solution.py:51
  118.5 13.7 %collective-permute-start.1 = (f32[4,32,512]{2,1,0:T(8,128)S(1)}, f32[4,32,512]{2,1,0:T(8,128)S(1)}, u32[]{:S(2)}, u32[]{:S(2)}) collective-permute-start(f32[4,32,512]{2,1,0:T(8,128)S(1)} %get-tuple-element.25), channel_id=1, source_target_pairs={{0,480},{1,33},{2,482},{3,35},{4,484},{5,37},{6,486},{7,39},{8,488... | collective-permute-start | bytes 786440 | tf_op jit(solution)/shard_map/ppermute | solution.py:51
  123.6 39.8 %collective-permute-start.13 = (f32[256,1280]{1,0:T(8,128)S(1)}, f32[256,1280]{1,0:T(8,128)S(1)}, u32[]{:S(2)}, u32[]{:S(2)}) collective-permute-start(f32[256,1280]{1,0:T(8,128)S(1)} %bitcast.30), channel_id=1, source_target_pairs={{0,1},{1,0},{2,3},{3,2},{4,5},{5,4},{6,7},{7,6},{8,9},{9,8},{10,11... | collective-permute-start | bytes 3932168 | tf_op jit(solution)/shard_map/ppermute | solution.py:180
  126.9 10.3 %collective-permute-start.6 = (f32[4,32,512]{2,1,0:T(8,128)S(1)}, f32[4,32,512]{2,1,0:T(8,128)S(1)}, u32[]{:S(2)}, u32[]{:S(2)}) collective-permute-start(f32[4,32,512]{2,1,0:T(8,128)S(1)} %get-tuple-element.23), channel_id=1, source_target_pairs={{0,480},{1,33},{2,482},{3,35},{4,484},{5,37},{6,486},{7,39},{8,488... | collective-permute-start | bytes 786440 | tf_op jit(solution)/shard_map/ppermute | solution.py:51
  132.3 9.1 %collective-permute-start.2 = (f32[2,32,512]{2,1,0:T(8,128)S(1)}, f32[2,32,512]{2,1,0:T(8,128)S(1)}, u32[]{:S(2)}, u32[]{:S(2)}) collective-permute-start(f32[2,32,512]{2,1,0:T(8,128)S(1)} %get-tuple-element.31), channel_id=1, source_target_pairs={{0,96},{1,417},{2,98},{3,419},{4,100},{5,421},{6,102},{7,423},{8,1... | collective-permute-start | bytes 393224 | tf_op jit(solution)/shard_map/ppermute | solution.py:51
  137.3 13.4 %collective-permute-start.7 = (f32[2,32,512]{2,1,0:T(8,128)S(1)}, f32[2,32,512]{2,1,0:T(8,128)S(1)}, u32[]{:S(2)}, u32[]{:S(2)}) collective-permute-start(f32[2,32,512]{2,1,0:T(8,128)S(1)} %get-tuple-element.29), channel_id=1, source_target_pairs={{0,96},{1,417},{2,98},{3,419},{4,100},{5,421},{6,102},{7,423},{8,1... | collective-permute-start | bytes 393224 | tf_op jit(solution)/shard_map/ppermute | solution.py:51
  141.4 13.9 %collective-permute-start.3 = (f32[1,32,512]{2,1,0:T(8,128)S(1)}, f32[1,32,512]{2,1,0:T(8,128)S(1)}, u32[]{:S(2)}, u32[]{:S(2)}) collective-permute-start(f32[1,32,512]{2,1,0:T(8,128)S(1)} %slice_add_fusion.10), channel_id=1, source_target_pairs={{0,352},{1,161},{2,354},{3,163},{4,356},{5,165},{6,358},{7,167},{8... | collective-permute-start | bytes 196616 | tf_op jit(solution)/shard_map/ppermute | solution.py:51
  150.7 12.6 %collective-permute-start.8 = (f32[1,32,512]{2,1,0:T(8,128)S(1)}, f32[1,32,512]{2,1,0:T(8,128)S(1)}, u32[]{:S(2)}, u32[]{:S(2)}) collective-permute-start(f32[1,32,512]{2,1,0:T(8,128)S(1)} %slice_add_fusion.8), channel_id=1, source_target_pairs={{0,352},{1,161},{2,354},{3,163},{4,356},{5,165},{6,358},{7,167},{8... | collective-permute-start | bytes 196616 | tf_op jit(solution)/shard_map/ppermute | solution.py:51
  166.2 14.0 %collective-permute-start.14 = (f32[1,32,512]{2,1,0:T(8,128)S(1)}, f32[1,32,512]{2,1,0:T(8,128)S(1)}, u32[]{:S(2)}, u32[]{:S(2)}) collective-permute-start(f32[1,32,512]{2,1,0:T(8,128)S(1)} %get-tuple-element.33), channel_id=1, source_target_pairs={{0,352},{1,161},{2,354},{3,163},{4,356},{5,165},{6,358},{7,167},{8... | collective-permute-start | bytes 196616 | tf_op jit(solution)/shard_map/ppermute | solution.py:66
  170.3 14.6 %collective-permute-start.18 = (f32[1,32,512]{2,1,0:T(8,128)S(1)}, f32[1,32,512]{2,1,0:T(8,128)S(1)}, u32[]{:S(2)}, u32[]{:S(2)}) collective-permute-start(f32[1,32,512]{2,1,0:T(8,128)S(1)} %get-tuple-element.32), channel_id=1, source_target_pairs={{0,352},{1,161},{2,354},{3,163},{4,356},{5,165},{6,358},{7,167},{8... | collective-permute-start | bytes 196616 | tf_op jit(solution)/shard_map/ppermute | solution.py:66
  180.3 9.0 %collective-permute-start.15 = (f32[2,32,512]{2,1,0:T(8,128)S(1)}, f32[2,32,512]{2,1,0:T(8,128)S(1)}, u32[]{:S(2)}, u32[]{:S(2)}) collective-permute-start(f32[2,32,512]{2,1,0:T(8,128)S(1)} %pad_maximum_fusion.6), channel_id=1, source_target_pairs={{0,96},{1,417},{2,98},{3,419},{4,100},{5,421},{6,102},{7,423},{8,1... | collective-permute-start | bytes 393224 | tf_op jit(solution)/shard_map/ppermute | solution.py:66
  184.9 11.3 %collective-permute-start.19 = (f32[2,32,512]{2,1,0:T(8,128)S(1)}, f32[2,32,512]{2,1,0:T(8,128)S(1)}, u32[]{:S(2)}, u32[]{:S(2)}) collective-permute-start(f32[2,32,512]{2,1,0:T(8,128)S(1)} %pad_maximum_fusion.7), channel_id=1, source_target_pairs={{0,96},{1,417},{2,98},{3,419},{4,100},{5,421},{6,102},{7,423},{8,1... | collective-permute-start | bytes 393224 | tf_op jit(solution)/shard_map/ppermute | solution.py:66
  189.3 11.0 %collective-permute-start.16 = (f32[4,32,512]{2,1,0:T(8,128)S(1)}, f32[4,32,512]{2,1,0:T(8,128)S(1)}, u32[]{:S(2)}, u32[]{:S(2)}) collective-permute-start(f32[4,32,512]{2,1,0:T(8,128)S(1)} %pad_maximum_fusion.4), channel_id=1, source_target_pairs={{0,480},{1,33},{2,482},{3,35},{4,484},{5,37},{6,486},{7,39},{8,488... | collective-permute-start | bytes 786440 | tf_op jit(solution)/shard_map/ppermute | solution.py:66
  196.3 11.9 %collective-permute-start.20 = (f32[4,32,512]{2,1,0:T(8,128)S(1)}, f32[4,32,512]{2,1,0:T(8,128)S(1)}, u32[]{:S(2)}, u32[]{:S(2)}) collective-permute-start(f32[4,32,512]{2,1,0:T(8,128)S(1)} %pad_maximum_fusion.5), channel_id=1, source_target_pairs={{0,480},{1,33},{2,482},{3,35},{4,484},{5,37},{6,486},{7,39},{8,488... | collective-permute-start | bytes 786440 | tf_op jit(solution)/shard_map/ppermute | solution.py:66
  200.3 13.8 %copy-start.1 = (f32[8,32,512]{2,1,0:T(8,128)}, f32[8,32,512]{2,1,0:T(8,128)S(1)}, u32[]{:S(2)}) copy-start(f32[8,32,512]{2,1,0:T(8,128)S(1)} %pad_maximum_fusion.2.held_ref) | copy-start | bytes 1572868
  200.4 13.7 %collective-permute-start.17 = (f32[8,32,512]{2,1,0:T(8,128)S(1)}, f32[8,32,512]{2,1,0:T(8,128)S(1)}, u32[]{:S(2)}, u32[]{:S(2)}) collective-permute-start(f32[8,32,512]{2,1,0:T(8,128)S(1)} %pad_maximum_fusion.2.held_ref), channel_id=1, source_target_pairs={{0,32},{1,481},{2,34},{3,483},{4,36},{5,485},{6,38},{7,487},{8,40}... | collective-permute-start | bytes 1572872 | tf_op jit(solution)/shard_map/ppermute | solution.py:66
  208.3 12.5 %copy-start.2 = (f32[8,32,512]{2,1,0:T(8,128)}, f32[8,32,512]{2,1,0:T(8,128)S(1)}, u32[]{:S(2)}) copy-start(f32[8,32,512]{2,1,0:T(8,128)S(1)} %pad_maximum_fusion.3.held_ref) | copy-start | bytes 1572868
  208.3 13.0 %collective-permute-start.21 = (f32[8,32,512]{2,1,0:T(8,128)S(1)}, f32[8,32,512]{2,1,0:T(8,128)S(1)}, u32[]{:S(2)}, u32[]{:S(2)}) collective-permute-start(f32[8,32,512]{2,1,0:T(8,128)S(1)} %pad_maximum_fusion.3.held_ref), channel_id=1, source_target_pairs={{0,32},{1,481},{2,34},{3,483},{4,36},{5,485},{6,38},{7,487},{8,40}... | collective-permute-start | bytes 1572872 | tf_op jit(solution)/shard_map/ppermute | solution.py:66
  214.1 0.8 copy-start.5
  221.2 0.8 copy-start.6
